TPU v7x, 128 devices: a whole 4x4x4 slice. The times are simulated.
128 devices in a mesh: rows: 16 (over z, y), cols: 8 (over x, core).
Axes of the slice: x: 4, y: 4, z: 4, core: 2. Of those that a mesh axis runs over, the one named last changes fastest.
Arguments:
- grad_stack: float32 [512, 64, 2048], P(None, 'rows', 'cols'), may hold values from -6 to 6
- moment_stack: float32 [512, 64, 2048], P(None, 'rows', 'cols'), may hold values from -6 to 6
- weight_stack: float32 [512, 64, 2048], P(None, 'rows', 'cols'), may hold values from -0.1875 to 0.1875
Outputs:
- new_weights: float32 [512, 64, 2048], P(None, 'rows', 'cols')
- new_momentum: float32 [512, 64, 2048], P(None, 'rows', 'cols')
All inputs are finite; a program needn't handle non-finite values.
Results may differ from a plain program's by a relative error of at most 0.0003.
Values sent between devices are 32-bit elements.
No kernel may reach another device: no remote copies, remote signals or barrier semaphores. Data moves between devices by JAX's collectives and lax.ppermute only.
A program may use at most 128 MiB of HBM per device.

v0:
```python
import jax
import jax.numpy as jnp
from jax import lax
from jax.sharding import PartitionSpec as P

ITERS = 5


hold_rate = 0.95
learn_rate = 1.0


def on_device(grad_stack, moment_stack, weight_stack):
    new_momentum = hold_rate * moment_stack + grad_stack
    moved = lax.all_to_all(new_momentum, "rows", split_axis=0, concat_axis=1, tiled=True)
    whole = lax.all_to_all(moved, "cols", split_axis=0, concat_axis=2, tiled=True)
    iterate = whole * lax.rsqrt(jnp.sum(whole * whole, axis=(1, 2), keepdims=True) + 1e-06)
    for step in range(ITERS):
        gram = jnp.einsum("mik,mjk->mij", iterate, iterate, precision=lax.Precision.HIGHEST)
        mixed = -4.775 * gram + 2.0315 * jnp.einsum(
            "mij,mjk->mik", gram, gram, precision=lax.Precision.HIGHEST
        )
        iterate = 3.4445 * iterate + jnp.einsum(
            "mij,mjk->mik", mixed, iterate, precision=lax.Precision.HIGHEST
        )
    iterate = lax.all_to_all(iterate, "cols", split_axis=2, concat_axis=0, tiled=True)
    back = lax.all_to_all(iterate, "rows", split_axis=1, concat_axis=0, tiled=True)
    new_weights = weight_stack - learn_rate * back
    return (new_weights, new_momentum)


def solution(mesh):
    placed = (P(None, "rows", "cols"), P(None, "rows", "cols"), P(None, "rows", "cols"))
    return jax.shard_map(
        on_device,
        mesh=mesh,
        in_specs=placed,
        out_specs=(P(None, "rows", "cols"), P(None, "rows", "cols")),
        check_vma=False,
    )
```

profile of v0, /device:TPU:0, one launch (start us, length us, event | category | flops | bytes accessed | tf_op | source)
XLA Modules:
  0.0 191.8 jit_solution(6366112335014375146)
XLA Ops:
  0.6 2.9 %multiply_add_fusion = f32[512,4,256]{2,1,0:T(4,128)S(1)} fusion(f32[512,4,256]{2,1,0:T(4,128)} %param.3, f32[512,4,256]{2,1,0:T(4,128)} %param.4), kind=kLoop, calls=%fused_computation.7 | loop fusion | flops 1048576 | bytes 6291456 | tf_op jit(solution)/shard_map/add | solution.py:14
  3.6 0.0 copy-start
  3.6 37.0 %all_to_all.72 = f32[512,4,256]{2,1,0:T(4,128)S(1)} all-to-all(f32[512,4,256]{2,1,0:T(4,128)S(1)} %multiply_add_fusion), channel_id=1, replica_groups=mesh['rows'=16,'cols'=8] {'rows'}, dimensions={0} | all-to-all | bytes 4194304 | tf_op jit(solution)/shard_map/all_to_all | solution.py:15
  40.6 0.0 copy-done
  40.6 0.4 copy.29
  41.0 0.2 copy.30
  41.2 1.2 copy.31
  42.4 31.4 %all_to_all.73 = f32[32,64,256]{2,1,0:T(8,128)S(1)} all-to-all(f32[32,64,256]{2,1,0:T(8,128)S(1)} %copy.31), channel_id=1, replica_groups=mesh['rows'=16,'cols'=8] {'cols'}, dimensions={0} | all-to-all | bytes 4194304 | tf_op jit(solution)/shard_map/all_to_all | solution.py:16
  73.8 0.3 copy.42
  74.1 0.3 multiply_reduce_fusion
  74.4 2.3 %fusion = f32[4,64,64]{2,1,0:T(8,128)S(1)} fusion(f32[4,64,2048]{2,1,0:T(8,128)S(1)} %bitcast.48, f32[4]{0:T(128)S(1)} %add_rsqrt_fusion), kind=kOutput, calls=%fused_computation.8 | convolution fusion | flops 403177472 | bytes 2162704 | tf_op jit(solution)/shard_map/mik,mjk->mij/dot_general | solution.py:19
  76.7 0.3 fusion.7
  77.0 2.1 %convolution_add_fusion.4 = f32[4,64,2048]{2,1,0:T(8,128)S(1)} fusion(f32[4,64,64]{2,1,0:T(8,128)S(1)} %fusion.7, f32[4,64,2048]{2,1,0:T(8,128)S(1)} %bitcast.49, f32[4]{0:T(128)S(1)} %add_rsqrt_fusion), kind=kOutput, calls=%fused_computation.4 | convolution fusion | flops 404750336 | bytes 4259856 | tf_op jit(solution)/shard_map/mij,mjk->mik/dot_general | solution.py:23
  79.1 2.1 %fusion.10 = f32[4,64,64]{2,1,0:T(8,128)S(1)} fusion(f32[4,64,2048]{2,1,0:T(8,128)S(1)} %convolution_add_fusion.4), kind=kOutput, calls=%fused_computation.24 | convolution fusion | flops 402653184 | bytes 2162688 | tf_op jit(solution)/shard_map/mik,mjk->mij/dot_general | solution.py:19
  81.1 0.3 fusion.6
  81.4 2.1 %convolution_add_fusion.3 = f32[4,64,2048]{2,1,0:T(8,128)S(1)} fusion(f32[4,64,64]{2,1,0:T(8,128)S(1)} %fusion.6, f32[4,64,2048]{2,1,0:T(8,128)S(1)} %convolution_add_fusion.4), kind=kOutput, calls=%fused_computation.3 | convolution fusion | flops 403701760 | bytes 4259840 | tf_op jit(solution)/shard_map/mij,mjk->mik/dot_general | solution.py:23
  83.5 2.1 %fusion.11 = f32[4,64,64]{2,1,0:T(8,128)S(1)} fusion(f32[4,64,2048]{2,1,0:T(8,128)S(1)} %convolution_add_fusion.3), kind=kOutput, calls=%fused_computation.25 | convolution fusion | flops 402653184 | bytes 2162688 | tf_op jit(solution)/shard_map/mik,mjk->mij/dot_general | solution.py:19
  85.6 0.3 fusion.5
  85.9 2.3 %convolution_add_fusion.2 = f32[4,64,2048]{2,1,0:T(8,128)S(1)} fusion(f32[4,64,64]{2,1,0:T(8,128)S(1)} %fusion.5, f32[4,64,2048]{2,1,0:T(8,128)S(1)} %convolution_add_fusion.3), kind=kOutput, calls=%fused_computation.2 | convolution fusion | flops 403701760 | bytes 4259840 | tf_op jit(solution)/shard_map/mij,mjk->mik/dot_general | solution.py:23
  88.2 2.1 %fusion.12 = f32[4,64,64]{2,1,0:T(8,128)S(1)} fusion(f32[4,64,2048]{2,1,0:T(8,128)S(1)} %convolution_add_fusion.2), kind=kOutput, calls=%fused_computation.26 | convolution fusion | flops 402653184 | bytes 2162688 | tf_op jit(solution)/shard_map/mik,mjk->mij/dot_general | solution.py:19
  90.3 0.3 fusion.4
  90.6 2.1 %convolution_add_fusion.1 = f32[4,64,2048]{2,1,0:T(8,128)S(1)} fusion(f32[4,64,64]{2,1,0:T(8,128)S(1)} %fusion.4, f32[4,64,2048]{2,1,0:T(8,128)S(1)} %convolution_add_fusion.2), kind=kOutput, calls=%fused_computation.1 | convolution fusion | flops 403701760 | bytes 4259840 | tf_op jit(solution)/shard_map/mij,mjk->mik/dot_general | solution.py:23
  92.7 2.1 %fusion.13 = f32[4,64,64]{2,1,0:T(8,128)S(1)} fusion(f32[4,64,2048]{2,1,0:T(8,128)S(1)} %convolution_add_fusion.1), kind=kOutput, calls=%fused_computation.27 | convolution fusion | flops 402653184 | bytes 2162688 | tf_op jit(solution)/shard_map/mik,mjk->mij/dot_general | solution.py:19
  94.8 0.3 fusion.3
  95.0 2.1 %convolution_add_fusion = f32[4,64,2048]{2,1,0:T(8,128)S(1)} fusion(f32[4,64,64]{2,1,0:T(8,128)S(1)} %fusion.3, f32[4,64,2048]{2,1,0:T(8,128)S(1)} %convolution_add_fusion.1), kind=kOutput, calls=%fused_computation | convolution fusion | flops 403701760 | bytes 4259840 | tf_op jit(solution)/shard_map/mij,mjk->mik/dot_general | solution.py:23
  97.1 3.2 %copy.33 = f32[4,64,2048]{1,0,2:T(4,128)} copy(f32[4,64,2048]{2,1,0:T(8,128)S(1)} %convolution_add_fusion) | data formatting | bytes 4194304 | tf_op jit(solution)/shard_map/add | solution.py:23
  100.3 6.8 %reshape.10 = f32[8,1,65536]{2,1,0:T(1,128)S(1)} reshape(f32[2048,4,64]{2,1,0:T(4,128)} %bitcast.52) | data formatting | bytes 4194304
  107.1 30.7 %all_to_all.74 = f32[8,1,65536]{2,1,0:T(1,128)} all-to-all(f32[8,1,65536]{2,1,0:T(1,128)S(1)} %reshape.10), channel_id=1, replica_groups=mesh['rows'=16,'cols'=8] {'cols'}, dimensions={0} | all-to-all | bytes 4194304 | tf_op jit(solution)/shard_map/all_to_all | solution.py:26
  137.8 0.5 broadcast.37
  138.3 7.2 %reduce.1 = f32[8,65536]{1,0:T(8,128)S(1)} reduce(f32[8,1,65536]{2,1,0:T(1,128)} %all_to_all.74, f32[]{:T(128)} %broadcast.37), dimensions={1}, to_apply=%all_to_all.60.reduce_sub_computation | reduce | bytes 4194308 | tf_op jit(solution)/shard_map/all_to_all | solution.py:26
  145.5 4.8 %reshape.11 = f32[2048,4,64]{2,1,0:T(4,128)} reshape(f32[8,65536]{1,0:T(8,128)S(1)} %reduce.1) | data formatting | bytes 4194304
  150.3 3.5 %copy.41 = f32[4,64,8,256]{3,1,0,2:T(8,128)S(1)} copy(f32[4,64,8,256]{1,0,3,2:T(4,128)} %bitcast.53) | data formatting | bytes 4194304 | tf_op jit(solution)/shard_map/all_to_all | solution.py:26
  153.8 1.2 copy.36
  155.1 31.6 %all_to_all.75 = f32[32,64,256]{2,0,1:T(8,128)S(1)} all-to-all(f32[32,64,256]{2,0,1:T(8,128)S(1)} %copy.36), channel_id=1, replica_groups=mesh['rows'=16,'cols'=8] {'rows'}, dimensions={1} | all-to-all | bytes 4194304 | tf_op jit(solution)/shard_map/all_to_all | solution.py:27
  186.6 0.0 copy-start.1
  186.6 0.2 copy.37
  186.9 1.3 copy-done.1
  188.2 0.4 bitcast_subtract_fusion
  188.7 2.7 %copy.39 = f32[512,4,256]{2,1,0:T(4,128)} copy(f32[512,4,256]{2,0,1:T(8,128)S(1)} %bitcast_subtract_fusion) | data formatting | bytes 4194304
  (1 shorter events, 0.0 us)
Async XLA Ops:
  3.6 37.0 %copy-start = (f32[512,4,256]{2,1,0:T(4,128)}, f32[512,4,256]{2,1,0:T(4,128)S(1)}, u32[]{:S(2)}) copy-start(f32[512,4,256]{2,1,0:T(4,128)S(1)} %multiply_add_fusion) | copy-start | bytes 6291460
  186.6 1.6 copy-start.1
where the time goes:
time: 195 us; the launch traced here: 192 us
  blocking collectives  131 us (67%)
  local copies, waits for them, and re-layouts  26.4 us (14%)
  matrix products  22.6 us (12%)
  other arithmetic  10.9 us (6%)
    all_to_all x1, blocking collectives, on_device(): lax.all_to_all(new_momentum, 'rows', split_axis=0, concat_axis=1, tiled=T...  37 us
    all_to_all x1, blocking collectives, on_device(): lax.all_to_all(iterate, 'rows', split_axis=1, concat_axis=0, tiled=True)  31.6 us
    all_to_all x1, blocking collectives, on_device(): lax.all_to_all(moved, 'cols', split_axis=0, concat_axis=2, tiled=True)  31.4 us
    all_to_all x1, blocking collectives, on_device(): lax.all_to_all(iterate, 'cols', split_axis=2, concat_axis=0, tiled=True)  30.7 us
    unnamed x7, local copies, waits for them, and re-layouts  15.6 us
    dot_general x5, matrix products, on_device(): jnp.einsum('mij,mjk->mik', mixed, iterate, precision=lax.Precision.HIGHEST)  10.7 us
    dot_general x5, matrix products, on_device(): jnp.einsum('mik,mjk->mij', iterate, iterate, precision=lax.Precision.HIGH...  10.6 us
    all_to_all x1, other arithmetic, on_device(): lax.all_to_all(iterate, 'cols', split_axis=2, concat_axis=0, tiled=True)  7.22 us

commit v1 on v0

v1 whole, which is shorter than its diff:
```python
import jax
import jax.numpy as jnp
from jax import lax
from jax.sharding import PartitionSpec as P

ITERS = 5


hold_rate = 0.95
learn_rate = 1.0


def dot(eq, a, b):
    return jnp.einsum(eq, a, b, precision=lax.Precision.HIGHEST)


def on_device(grad_stack, moment_stack, weight_stack):
    new_momentum = hold_rate * moment_stack + grad_stack
    rows_in = lax.all_to_all(new_momentum, "rows", split_axis=0, concat_axis=1, tiled=True)
    part = dot("mik,mjk->mij", rows_in, rows_in)
    n = part.shape[0]
    packed = jnp.concatenate([part[: n // 2], part[n // 2 :]], axis=2)
    parts = lax.all_to_all(packed, "cols", split_axis=0, concat_axis=0, tiled=True)
    k = lax.axis_size("cols")
    total = jnp.sum(parts.reshape(k, n // 2 // k, 64, 128), axis=0)
    gram = jnp.concatenate([total[:, :, :64], total[:, :, 64:]], axis=0)
    size = jnp.trace(gram, axis1=1, axis2=2)[:, None, None] + 1e-06
    gram = gram / size
    eye = jnp.eye(64, dtype=jnp.float32)
    left = lax.rsqrt(size) * eye
    for step in range(ITERS):
        square = dot("mij,mjk->mik", gram, gram)
        poly = 3.4445 * eye - 4.775 * gram + 2.0315 * square
        left = dot("mij,mjk->mik", poly, left)
        if step + 1 < ITERS:
            gram = dot("mij,mjk->mik", poly, dot("mij,mjk->mik", gram, poly))
            gram = 0.5 * (gram + jnp.swapaxes(gram, 1, 2))
    packed = jnp.concatenate([left[: n // 2 // k], left[n // 2 // k :]], axis=2)
    lefts = lax.all_gather(packed, "cols", axis=0, tiled=True)
    lefts = jnp.concatenate([lefts[:, :, :64], lefts[:, :, 64:]], axis=0)
    iterate = dot("mij,mjk->mik", lefts, rows_in)
    back = lax.all_to_all(iterate, "rows", split_axis=1, concat_axis=0, tiled=True)
    new_weights = weight_stack - learn_rate * back
    return (new_weights, new_momentum)


def solution(mesh):
    placed = (P(None, "rows", "cols"), P(None, "rows", "cols"), P(None, "rows", "cols"))
    return jax.shard_map(
        on_device,
        mesh=mesh,
        in_specs=placed,
        out_specs=(P(None, "rows", "cols"), P(None, "rows", "cols")),
        check_vma=False,
    )
```

time: 195 us -> 123 us (0.63); the launches traced: 192 us -> 122 us
  blocking collectives: 131 us -> 83.6 us
  local copies, waits for them, and re-layouts: 26.4 us -> 7.44 us
  matrix products: 22.6 us -> 8.94 us
  waiting for transfers between devices: 0 us -> 10.5 us
  other arithmetic: 10.9 us -> 6.21 us
  starting transfers between devices: 0 us -> 4.3 us
    all_to_all x2 -> x0, blocking collectives: 62.1 us -> none  [the longest x1 31.4 us: on_device(): lax.all_to_all(moved, 'cols', split_axis=0, concat_axis=2, tiled=True)]
    unnamed x7 -> x4, local copies, waits for them, and re-layouts: 15.6 us -> 0.19 us
    dot_general x15 -> x20, matrix products: 22.6 us -> 8.94 us  [dot(): return jnp.einsum(eq, a, b, precision=lax.Precision.HIGHEST)]
    all_gather x0 -> x1, blocking collectives: none -> 13.3 us  [on_device(): lefts = lax.all_gather(packed, 'cols', axis=0, tiled=True)]
    all_to_all x0 -> x1, waiting for transfers between devices: none -> 10.5 us  [on_device(): lax.all_to_all(packed, 'cols', split_axis=0, concat_axis=0, tiled=True)]
    all_to_all x1 -> x0, other arithmetic: 7.22 us -> none  [on_device(): lax.all_to_all(iterate, 'cols', split_axis=2, concat_axis=0, tiled=True)]
    all_to_all x4 -> x0, local copies, waits for them, and re-layouts: 5.51 us -> none  [the longest x3 5.24 us: on_device(): lax.all_to_all(iterate, 'cols', split_axis=2, concat_axis=0, tiled=True)]
    all_to_all x0 -> x1, starting transfers between devices: none -> 4.3 us  [on_device(): lax.all_to_all(packed, 'cols', split_axis=0, concat_axis=0, tiled=True)]
  transfers between devices with their start and end apart: 0 -> 1, of which waited for: 0 -> 1; matrix products, arithmetic and copies ran while one was open for 0% -> 0% of each run, Pallas kernels for 0% -> 0%
where the time goes in v1:
time: 123 us; the launch traced here: 122 us
  blocking collectives  83.6 us (68%)
  waiting for transfers between devices  10.5 us (9%)
  matrix products  8.94 us (7%)
  local copies, waits for them, and re-layouts  7.44 us (6%)
  other arithmetic  6.21 us (5%)
  starting transfers between devices  4.3 us (3%)
    all_to_all x1, blocking collectives, on_device(): lax.all_to_all(new_momentum, 'rows', split_axis=0, concat_axis=1, tiled=T...  37 us
    all_to_all x1, blocking collectives, on_device(): lax.all_to_all(iterate, 'rows', split_axis=1, concat_axis=0, tiled=True)  33.4 us
    all_gather x1, blocking collectives, on_device(): lefts = lax.all_gather(packed, 'cols', axis=0, tiled=True)  13.3 us
    all_to_all x1, waiting for transfers between devices, on_device(): lax.all_to_all(packed, 'cols', split_axis=0, concat_axis=0, tiled=True)  10.5 us
    dot_general x20, matrix products, dot(): return jnp.einsum(eq, a, b, precision=lax.Precision.HIGHEST)  8.94 us
    all_to_all x1, starting transfers between devices, on_device(): lax.all_to_all(packed, 'cols', split_axis=0, concat_axis=0, tiled=True)  4.3 us
    all_to_all x2, local copies, waits for them, and re-layouts, on_device(): lax.all_to_all(new_momentum, 'rows', split_axis=0, concat_axis=1, tiled=T...  3.88 us
    add x1, other arithmetic, on_device(): new_momentum = hold_rate * moment_stack + grad_stack  2.94 us
  transfers between devices with their start and end apart: 1, of which 1 were waited for; matrix products, arithmetic and copies ran while one was open for 0% of the time, Pallas kernels for 0%

profile of v1, /device:TPU:0, one launch (start us, length us, event | category | flops | bytes accessed | tf_op | source)
XLA Modules:
  0.0 121.9 jit_solution(11145713196418754118)
XLA Ops:
  0.6 2.9 %multiply_add_fusion = f32[512,4,256]{2,1,0:T(4,128)S(1)} fusion(f32[512,4,256]{2,1,0:T(4,128)} %param.3, f32[512,4,256]{2,1,0:T(4,128)} %param.4), kind=kLoop, calls=%fused_computation.2 | loop fusion | flops 1048576 | bytes 6291456 | tf_op jit(solution)/shard_map/add | solution.py:18
  3.6 0.0 copy-start
  3.6 37.0 %all_to_all.41 = f32[512,4,256]{2,1,0:T(4,128)S(1)} all-to-all(f32[512,4,256]{2,1,0:T(4,128)S(1)} %multiply_add_fusion), channel_id=1, replica_groups=mesh['rows'=16,'cols'=8] {'rows'}, dimensions={0} | all-to-all | bytes 4194304 | tf_op jit(solution)/shard_map/all_to_all | solution.py:19
  40.6 0.0 copy-done
  40.6 1.9 %copy.19 = f32[16,32,4,256]{3,2,0,1:T(4,128)} copy(f32[16,32,4,256]{3,2,1,0:T(4,128)S(1)} %bitcast.77) | data formatting | bytes 4194304 | tf_op jit(solution)/shard_map/all_to_all | solution.py:19
  42.5 2.0 %all_to_all.32 = f32[32,64,256]{2,1,0:T(8,128)S(1)} reshape(f32[32,16,4,256]{3,2,1,0:T(4,128)} %bitcast.75) | data formatting | bytes 4194304 | tf_op jit(solution)/shard_map/all_to_all | solution.py:19
  44.4 2.1 %fusion.49 = f32[32,64,64]{2,1,0:T(8,128)S(1)} fusion(f32[32,64,256]{2,1,0:T(8,128)S(1)} %all_to_all.32), kind=kOutput, calls=%fused_computation.65 | convolution fusion | flops 402653184 | bytes 2621440 | tf_op jit(solution)/shard_map/mik,mjk->mij/dot_general | solution.py:14
  46.6 0.1 fusion.45
  46.6 1.0 pad_maximum_fusion
  47.6 4.3 %all-to-all-start.1 = ((f32[16,64,128]{2,1,0:T(8,128)}), f32[16,64,128]{2,1,0:T(8,128)S(1)}, u32[]{:S(2)}, u32[]{:S(2)}) async-start(f32[16,64,128]{2,1,0:T(8,128)} %pad_maximum_fusion), calls=%async_computation.1 | async-start | bytes 1048576 | tf_op jit(solution)/shard_map/all_to_all | solution.py:23
  52.0 10.5 %all-to-all-done.1 = f32[16,64,128]{2,1,0:T(8,128)S(1)} async-done(((f32[16,64,128]{2,1,0:T(8,128)}), f32[16,64,128]{2,1,0:T(8,128)S(1)}, u32[]{:S(2)}, u32[]{:S(2)}) %all-to-all-start.1) | async-done | bytes 524320 | tf_op jit(solution)/shard_map/all_to_all | solution.py:23
  62.5 0.1 fusion.48
  62.6 0.1 select_reduce_fusion
  62.7 0.3 fusion.4
  63.1 0.3 fusion.43
  63.4 0.3 fusion.50
  63.7 0.1 copy.12
  63.8 0.3 fusion.3
  64.0 0.3 fusion.18
  64.3 0.3 fusion.51
  64.6 0.3 fusion.9
  64.9 0.3 fusion.54
  65.2 0.1 copy.13
  65.3 0.3 fusion.2
  65.5 0.3 fusion.15
  65.8 0.3 fusion.52
  66.1 0.3 fusion.55
  66.3 0.1 copy.14
  66.4 0.3 fusion.1
  66.7 0.3 fusion.12
  67.0 0.3 fusion.53
  67.2 0.3 fusion.56
  67.5 0.1 copy.15
  67.6 0.3 fusion
  67.9 0.3 fusion.57
  68.2 0.1 pad_maximum_fusion.2
  68.2 13.3 %all_gather.3 = f32[16,64,128]{2,1,0:T(8,128)S(1)} all-gather(f32[2,64,128]{2,1,0:T(8,128)S(1)} %pad_maximum_fusion.2), channel_id=1, replica_groups=mesh['rows'=16,'cols'=8] {'cols'}, dimensions={0}, use_global_device_ids=true | all-gather | bytes 589824 | tf_op jit(solution)/shard_map/all_gather | solution.py:39
  81.5 0.2 fusion.46
  81.7 2.0 %fusion.5 = f32[32,64,256]{2,1,0:T(8,128)S(1)} fusion(f32[32,64,256]{2,1,0:T(8,128)S(1)} %all_to_all.32, f32[16,64,64]{2,1,0:T(8,128)S(1)} %get-tuple-element.5, f32[16,64,64]{2,1,0:T(8,128)S(1)} %get-tuple-element.4), kind=kOutput, calls=%fused_computation.13 | convolution fusion | flops 402784256 | bytes 4718592 | tf_op jit(solution)/shard_map/mij,mjk->mik/dot_general | solution.py:14
  83.7 1.2 copy.16
  84.9 33.4 %all_to_all.42 = f32[32,64,256]{2,0,1:T(8,128)S(1)} all-to-all(f32[32,64,256]{2,0,1:T(8,128)S(1)} %copy.16), channel_id=1, replica_groups=mesh['rows'=16,'cols'=8] {'rows'}, dimensions={1} | all-to-all | bytes 4194304 | tf_op jit(solution)/shard_map/all_to_all | solution.py:42
  118.3 0.0 copy-start.1
  118.3 1.4 %copy.17 = f32[16,32,4,256]{3,2,1,0:T(4,128)S(1)} copy(f32[16,32,4,256]{3,1,2,0:T(8,128)S(1)} %bitcast.76) | data formatting | bytes 4194304 | tf_op jit(solution)/shard_map/all_to_all | solution.py:42
  119.7 0.2 copy-done.1
  119.9 2.0 %bitcast_subtract_fusion = f32[512,4,256]{2,1,0:T(4,128)} fusion(f32[512,4,256]{2,1,0:T(4,128)S(1)} %copy-done.1, f32[16,32,4,256]{3,2,1,0:T(4,128)S(1)} %copy.17), kind=kLoop, calls=%fused_computation | loop fusion | flops 524288 | bytes 6291456 | tf_op jit(solution)/shard_map/sub | solution.py:43
  (6 shorter events, 0.1 us)
Async XLA Ops:
  3.6 37.0 %copy-start = (f32[512,4,256]{2,1,0:T(4,128)}, f32[512,4,256]{2,1,0:T(4,128)S(1)}, u32[]{:S(2)}) copy-start(f32[512,4,256]{2,1,0:T(4,128)S(1)} %multiply_add_fusion) | copy-start | bytes 6291460
  47.6 14.8 %all-to-all-start.1 = ((f32[16,64,128]{2,1,0:T(8,128)}), f32[16,64,128]{2,1,0:T(8,128)S(1)}, u32[]{:S(2)}, u32[]{:S(2)}) async-start(f32[16,64,128]{2,1,0:T(8,128)} %pad_maximum_fusion), calls=%async_computation.1 | async-start | bytes 1048576 | tf_op jit(solution)/shard_map/all_to_all | solution.py:23
  118.3 1.6 %copy-start.1 = (f32[512,4,256]{2,1,0:T(4,128)S(1)}, f32[512,4,256]{2,1,0:T(4,128)}, u32[]{:S(2)}) copy-start(f32[512,4,256]{2,1,0:T(4,128)} %param.5) | copy-start | bytes 6291460

commit v2 on v0

v2 whole, which is shorter than its diff:
```python
import jax
import jax.numpy as jnp
from jax import lax
from jax.experimental import pallas as pl
from jax.experimental.pallas import tpu as pltpu
from jax.sharding import PartitionSpec as P

ITERS = 5


hold_rate = 0.95
learn_rate = 1.0


def dot(a, b):
    return lax.dot_general(
        a, b, (((1,), (0,)), ((), ())),
        precision=lax.Precision.HIGHEST, preferred_element_type=jnp.float32,
    )


def dot_t(a, b):
    return lax.dot_general(
        a, b, (((1,), (1,)), ((), ())),
        precision=lax.Precision.HIGHEST, preferred_element_type=jnp.float32,
    )


def orthogonal(rows, cols, mats):
    def body(in_ref, out_ref, x_ref, left_ref):
        here, wide = in_ref.shape[1], in_ref.shape[2]
        side = here * rows
        for m in range(mats):
            for r in range(0, rows, 2):
                for c in range(cols):
                    top = in_ref[(r * cols + c) * mats + m]
                    low = in_ref[((r + 1) * cols + c) * mats + m]
                    x_ref[m, pl.ds(r * here, 2 * here), pl.ds(c * wide, wide)] = jnp.concatenate([top, low], axis=0)
        at_row = lax.broadcasted_iota(jnp.int32, (side, side), 0)
        at_col = lax.broadcasted_iota(jnp.int32, (side, side), 1)
        eye = jnp.where(at_row == at_col, 1.0, 0.0).astype(jnp.float32)
        grams, lefts = [], []
        for m in range(mats):
            x = x_ref[m]
            gram = dot_t(x, x)
            size = jnp.sum(gram * eye, axis=(0, 1), keepdims=True) + 1e-06
            grams.append(gram / size)
            lefts.append(lax.rsqrt(size) * eye)
        for step in range(ITERS):
            squares = [dot(g, g) for g in grams]
            polys = [3.4445 * eye - 4.775 * g + 2.0315 * s for g, s in zip(grams, squares)]
            lefts = [dot(p, q) for p, q in zip(polys, lefts)]
            if step + 1 < ITERS:
                halves = [dot(g, p) for g, p in zip(grams, polys)]
                grams = [dot(p, h) for p, h in zip(polys, halves)]
                grams = [0.5 * (g + g.T) for g in grams]
        for m in range(mats):
            y = dot(lefts[m], x_ref[m])
            for r in range(rows):
                for c in range(cols):
                    out_ref[(r * cols + c) * mats + m] = y[r * here : (r + 1) * here, c * wide : (c + 1) * wide]

    def call(pieces):
        n, here, wide = pieces.shape
        return pl.pallas_call(
            body,
            out_shape=jax.ShapeDtypeStruct(pieces.shape, pieces.dtype),
            in_specs=[pl.BlockSpec(memory_space=pltpu.VMEM)],
            out_specs=pl.BlockSpec(memory_space=pltpu.VMEM),
            scratch_shapes=[
                pltpu.VMEM((mats, here * rows, wide * cols), jnp.float32),
                pltpu.VMEM((mats, here * rows, here * rows), jnp.float32),
            ],
            compiler_params=pltpu.CompilerParams(vmem_limit_bytes=32 * 1024 * 1024),
            name="orthogonal",
        )(pieces)

    return call


def on_device(grad_stack, moment_stack, weight_stack):
    axes = ("rows", "cols")
    rows, cols = lax.axis_size("rows"), lax.axis_size("cols")
    new_momentum = hold_rate * moment_stack + grad_stack
    pieces = lax.all_to_all(new_momentum, axes, split_axis=0, concat_axis=0, tiled=True)
    pieces = orthogonal(rows, cols, pieces.shape[0] // (rows * cols))(pieces)
    back = lax.all_to_all(pieces, axes, split_axis=0, concat_axis=0, tiled=True)
    new_weights = weight_stack - learn_rate * back
    return (new_weights, new_momentum)


def solution(mesh):
    placed = (P(None, "rows", "cols"), P(None, "rows", "cols"), P(None, "rows", "cols"))
    return jax.shard_map(
        on_device,
        mesh=mesh,
        in_specs=placed,
        out_specs=(P(None, "rows", "cols"), P(None, "rows", "cols")),
        check_vma=False,
    )
```

time: 195 us -> 91.4 us (0.47); the launches traced: 192 us -> 91.2 us
  blocking collectives: 131 us -> 78.9 us
  local copies, waits for them, and re-layouts: 26.4 us -> 0.01 us
  matrix products: 22.6 us -> 0 us
  Pallas kernels: 0 us -> 6.86 us
  other arithmetic: 10.9 us -> 4.8 us
    all_to_all x4 -> x2, blocking collectives: 131 us -> 78.9 us  [the longest x1 42.9 us: on_device(): lax.all_to_all(new_momentum, axes, split_axis=0, concat_axis=0, tiled=True)]
    dot_general x15 -> x0, matrix products: 22.6 us -> none  [the longest x5 10.7 us: on_device(): jnp.einsum('mij,mjk->mik', mixed, iterate, precision=lax.Precision.HIGHEST)]
    unnamed x7 -> x4, local copies, waits for them, and re-layouts: 15.6 us -> 0.01 us
    all_to_all x8 -> x0, local copies, waits for them, and re-layouts: 7.61 us -> none  [the longest x3 5.24 us: on_device(): lax.all_to_all(iterate, 'cols', split_axis=2, concat_axis=0, tiled=True)]
    all_to_all x1 -> x0, other arithmetic: 7.22 us -> none  [on_device(): lax.all_to_all(iterate, 'cols', split_axis=2, concat_axis=0, tiled=True)]
    pallas_call x0 -> x1, Pallas kernels: none -> 6.86 us  [call(): pl.pallas_call(body, out_shape=jax.ShapeDtypeStruct(pieces.shape, pieces....]
    add x1 -> x0, local copies, waits for them, and re-layouts: 3.17 us -> none  [on_device(): 3.4445 * iterate]
where the time goes in v2:
time: 91.4 us; the launch traced here: 91.2 us
  blocking collectives  78.9 us (86%)
  Pallas kernels  6.86 us (8%)
  other arithmetic  4.8 us (5%)
    all_to_all x1, blocking collectives, on_device(): lax.all_to_all(new_momentum, axes, split_axis=0, concat_axis=0, tiled=True)  42.9 us
    all_to_all x1, blocking collectives, on_device(): back = lax.all_to_all(pieces, axes, split_axis=0, concat_axis=0, tiled=True)  36 us
    pallas_call x1, Pallas kernels, call(): pl.pallas_call(body, out_shape=jax.ShapeDtypeStruct(pieces.shape, pieces....  6.86 us
    add x1, other arithmetic, on_device(): new_momentum = hold_rate * moment_stack + grad_stack  2.94 us
    sub x1, other arithmetic, on_device(): new_weights = weight_stack - learn_rate * back  1.86 us

profile of v2, /device:TPU:0, one launch (start us, length us, event | category | flops | bytes accessed | tf_op | source)
XLA Modules:
  0.0 91.2 jit_solution(7587582305404640340)
XLA Ops:
  0.6 2.9 %multiply_add_fusion = f32[512,4,256]{2,1,0:T(4,128)S(1)} fusion(f32[512,4,256]{2,1,0:T(4,128)} %param.3, f32[512,4,256]{2,1,0:T(4,128)} %param.4), kind=kLoop, calls=%fused_computation | loop fusion | flops 1048576 | bytes 6291456 | tf_op jit(solution)/shard_map/add | solution.py:84
  3.6 0.0 copy-start
  3.6 42.9 %all_to_all.10.in_ref = f32[512,4,256]{2,1,0:T(4,128)S(1)} all-to-all(f32[512,4,256]{2,1,0:T(4,128)S(1)} %multiply_add_fusion), channel_id=1, replica_groups=mesh['rows'=16,'cols'=8] {'rows','cols'}, dimensions={0} | all-to-all | bytes 4194304 | tf_op jit(solution)/shard_map/all_to_all | solution.py:85
  46.5 6.9 %orthogonal.1 = f32[512,4,256]{2,1,0:T(4,128)S(1)} custom-call(f32[512,4,256]{2,1,0:T(4,128)S(1)} %all_to_all.10.in_ref), custom_call_target="tpu_custom_call" | custom-call | tf_op jit(solution)/shard_map/orthogonal/pallas_call | solution.py:65
  53.3 0.0 copy-done
  53.3 0.0 copy-start.1
  53.3 36.0 %all_to_all.11 = f32[512,4,256]{2,1,0:T(4,128)S(1)} all-to-all(f32[512,4,256]{2,1,0:T(4,128)S(1)} %orthogonal.1), channel_id=1, replica_groups=mesh['rows'=16,'cols'=8] {'rows','cols'}, dimensions={0} | all-to-all | bytes 4194304 | tf_op jit(solution)/shard_map/all_to_all | solution.py:87
  89.3 0.0 copy-done.1
  89.3 1.9 %sub.3 = f32[512,4,256]{2,1,0:T(4,128)} subtract(f32[512,4,256]{2,1,0:T(4,128)S(1)} %copy-done.1, f32[512,4,256]{2,1,0:T(4,128)S(1)} %all_to_all.11) | non-fusion elementwise | flops 524288 | bytes 6291456 | tf_op jit(solution)/shard_map/sub | solution.py:88
Async XLA Ops:
  3.6 49.8 %copy-start = (f32[512,4,256]{2,1,0:T(4,128)}, f32[512,4,256]{2,1,0:T(4,128)S(1)}, u32[]{:S(2)}) copy-start(f32[512,4,256]{2,1,0:T(4,128)S(1)} %multiply_add_fusion) | copy-start | bytes 6291460
  53.3 36.0 %copy-start.1 = (f32[512,4,256]{2,1,0:T(4,128)S(1)}, f32[512,4,256]{2,1,0:T(4,128)}, u32[]{:S(2)}) copy-start(f32[512,4,256]{2,1,0:T(4,128)} %param.5) | copy-start | bytes 6291460

commit v3 on v2

v3 whole, which is shorter than its diff:
```python
import jax
import jax.numpy as jnp
from jax import lax
from jax.experimental import pallas as pl
from jax.experimental.pallas import tpu as pltpu
from jax.sharding import PartitionSpec as P

ITERS = 5
RESTART = 3


hold_rate = 0.95
learn_rate = 1.0

F32, BF16 = jnp.float32, jnp.bfloat16


def split3(value):
    high = value.astype(BF16)
    rest = value - high.astype(F32)
    mid = rest.astype(BF16)
    return high, mid, (rest - mid.astype(F32)).astype(BF16)


def dot(a, b):
    return lax.dot_general(a, b, (((1,), (0,)), ((), ())), preferred_element_type=F32)


def dot_t(a, b):
    return lax.dot_general(a, b, (((1,), (1,)), ((), ())), preferred_element_type=F32)


def orthogonal(rows, cols, mats):
    def body(in_ref, out_ref, x_ref):
        here, wide = in_ref.shape[1], in_ref.shape[2]
        side = here * rows
        lane = lax.broadcasted_iota(jnp.int32, (side, 2 * side), 1)
        row = lax.broadcasted_iota(jnp.int32, (side, 2 * side), 0)
        eye = jnp.where((lane == row) | (lane == row + side), 1.0, 0.0).astype(F32)
        eye_one = eye[:, :side]
        first = jnp.where(lane < side, 1.0, 0.0).astype(BF16)
        second = jnp.where(lane < side, 0.0, 1.0).astype(BF16)

        def keep(m, top, at, value):
            for k, term in enumerate(split3(value)):
                x_ref[m, pl.ds(k * side + top, value.shape[0]), pl.ds(at, value.shape[1])] = term

        def gram_of(m):
            c = dot_t(x_ref[m, : 2 * side], x_ref[m])
            half = c[:side, side : 2 * side] + (c[:side, 2 * side :] + 0.5 * c[side:, side : 2 * side])
            return c[:side, :side] + (half + half.T)

        def streamed(value):
            v1, v2, v3 = split3(value)
            return jnp.concatenate([v1, v1, v1, v2, v2, v3], axis=1)

        def held(value):
            v1, v2, v3 = [jnp.concatenate([v * first, v * second], axis=0) for v in split3(value)]
            return jnp.concatenate([v1, v2, v3, v1, v2, v1], axis=0)

        def steps(grams, lefts, count):
            pairs = range(len(grams))
            for step in range(count):
                gram_held = [held(g) for g in grams]
                squares = [dot(streamed(grams[p]), gram_held[p]) for p in pairs]
                polys = [3.4445 * eye - 4.775 * grams[p] + 2.0315 * squares[p] for p in pairs]
                flow = [streamed(poly) for poly in polys]
                last = step + 1 == count
                if step == 0:
                    mixed = None if last else [dot(flow[p], gram_held[p]) for p in pairs]
                    lefts = [polys[p] if lefts is None else polys[p] * lefts[p] for p in pairs]
                elif last:
                    lefts = [dot(flow[p], held(lefts[p])) for p in pairs]
                else:
                    both = [dot(flow[p], jnp.concatenate([held(lefts[p]), gram_held[p]], axis=1)) for p in pairs]
                    lefts = [b[:, : 2 * side] for b in both]
                    mixed = [b[:, 2 * side :] for b in both]
                if not last:
                    grams = [dot(streamed(mixed[p]), held(polys[p])) for p in pairs]
            return lefts

        def weights_of(lefts, m):
            left = lefts[m // 2][:, (m % 2) * side : (m % 2 + 1) * side]
            q1, q2, q3 = split3(left)
            none = jnp.zeros((side, 2 * side), BF16)
            return jnp.concatenate(
                [jnp.concatenate([q1, q1, q1, q2], axis=1), jnp.concatenate([q3, q2, none], axis=1)], axis=0
            )

        def applied(weights, m, at):
            terms = x_ref[m, :, pl.ds(at, wide)]
            got = dot(weights, jnp.concatenate([terms, terms[:side]], axis=0))
            return got[:side] + got[side:]

        def pair_up(values):
            return [jnp.concatenate(values[m : m + 2], axis=1) for m in range(0, mats, 2)]

        for m in range(mats):
            for r in range(0, rows, 4):
                for c in range(cols):
                    piece = [in_ref[((r + k) * cols + c) * mats + m] for k in range(4)]
                    keep(m, r * here, c * wide, jnp.concatenate(piece, axis=0))
        grams = [gram_of(m) for m in range(mats)]
        sizes = [jnp.sum(g * eye_one, axis=(0, 1), keepdims=True) + 1e-06 for g in grams]
        scales = [jnp.broadcast_to(lax.rsqrt(s), (side, side)) for s in sizes]
        grams = [g / s for g, s in zip(grams, sizes)]
        lefts = steps(pair_up(grams), pair_up(scales), RESTART)
        for m in range(mats):
            weights = weights_of(lefts, m)
            for c in range(cols):
                keep(m, 0, c * wide, applied(weights, m, c * wide))
        lefts = steps(pair_up([gram_of(m) for m in range(mats)]), None, ITERS - RESTART)
        for m in range(mats):
            weights = weights_of(lefts, m)
            for c in range(cols):
                y = applied(weights, m, c * wide)
                for r in range(rows):
                    out_ref[(r * cols + c) * mats + m] = y[r * here : (r + 1) * here]

    def call(pieces):
        n, here, wide = pieces.shape
        return pl.pallas_call(
            body,
            out_shape=jax.ShapeDtypeStruct(pieces.shape, pieces.dtype),
            in_specs=[pl.BlockSpec(memory_space=pltpu.VMEM)],
            out_specs=pl.BlockSpec(memory_space=pltpu.VMEM),
            scratch_shapes=[pltpu.VMEM((mats, 3 * here * rows, wide * cols), BF16)],
            compiler_params=pltpu.CompilerParams(vmem_limit_bytes=32 * 1024 * 1024),
            name="orthogonal",
        )(pieces)

    return call


def on_device(grad_stack, moment_stack, weight_stack):
    axes = ("rows", "cols")
    rows, cols = lax.axis_size("rows"), lax.axis_size("cols")
    new_momentum = hold_rate * moment_stack + grad_stack
    pieces = lax.all_to_all(new_momentum, axes, split_axis=0, concat_axis=0, tiled=True)
    pieces = orthogonal(rows, cols, pieces.shape[0] // (rows * cols))(pieces)
    back = lax.all_to_all(pieces, axes, split_axis=0, concat_axis=0, tiled=True)
    new_weights = weight_stack - learn_rate * back
    return (new_weights, new_momentum)


def solution(mesh):
    placed = (P(None, "rows", "cols"), P(None, "rows", "cols"), P(None, "rows", "cols"))
    return jax.shard_map(
        on_device,
        mesh=mesh,
        in_specs=placed,
        out_specs=(P(None, "rows", "cols"), P(None, "rows", "cols")),
        check_vma=False,
    )
```

time: 91.4 us -> 91.4 us (level)
  no operation moved by 1% of the time
where the time goes in v3:
time: 91.4 us; the launch traced here: 91.2 us
  blocking collectives  78.9 us (86%)
  Pallas kernels  6.9 us (8%)
  other arithmetic  4.8 us (5%)
    all_to_all x1, blocking collectives, on_device(): lax.all_to_all(new_momentum, axes, split_axis=0, concat_axis=0, tiled=True)  42.9 us
    all_to_all x1, blocking collectives, on_device(): back = lax.all_to_all(pieces, axes, split_axis=0, concat_axis=0, tiled=True)  36 us
    pallas_call x1, Pallas kernels, call(): pl.pallas_call(body, out_shape=jax.ShapeDtypeStruct(pieces.shape, pieces....  6.9 us
    add x1, other arithmetic, on_device(): new_momentum = hold_rate * moment_stack + grad_stack  2.94 us
    sub x1, other arithmetic, on_device(): new_weights = weight_stack - learn_rate * back  1.86 us

profile of v3, /device:TPU:0, one launch (start us, length us, event | category | flops | bytes accessed | tf_op | source)
XLA Modules:
  0.0 91.2 jit_solution(16553719444508687642)
XLA Ops:
  0.6 2.9 %multiply_add_fusion = f32[512,4,256]{2,1,0:T(4,128)S(1)} fusion(f32[512,4,256]{2,1,0:T(4,128)} %param.3, f32[512,4,256]{2,1,0:T(4,128)} %param.4), kind=kLoop, calls=%fused_computation | loop fusion | flops 1048576 | bytes 6291456 | tf_op jit(solution)/shard_map/add | solution.py:138
  3.6 0.0 copy-start
  3.6 42.9 %all_to_all.10.in_ref = f32[512,4,256]{2,1,0:T(4,128)S(1)} all-to-all(f32[512,4,256]{2,1,0:T(4,128)S(1)} %multiply_add_fusion), channel_id=1, replica_groups=mesh['rows'=16,'cols'=8] {'rows','cols'}, dimensions={0} | all-to-all | bytes 4194304 | tf_op jit(solution)/shard_map/all_to_all | solution.py:139
  46.5 6.9 %orthogonal.1 = f32[512,4,256]{2,1,0:T(4,128)S(1)} custom-call(f32[512,4,256]{2,1,0:T(4,128)S(1)} %all_to_all.10.in_ref), custom_call_target="tpu_custom_call" | custom-call | tf_op jit(solution)/shard_map/orthogonal/pallas_call | solution.py:122
  53.4 0.0 copy-done
  53.4 0.0 copy-start.1
  53.4 36.0 %all_to_all.11 = f32[512,4,256]{2,1,0:T(4,128)S(1)} all-to-all(f32[512,4,256]{2,1,0:T(4,128)S(1)} %orthogonal.1), channel_id=1, replica_groups=mesh['rows'=16,'cols'=8] {'rows','cols'}, dimensions={0} | all-to-all | bytes 4194304 | tf_op jit(solution)/shard_map/all_to_all | solution.py:141
  89.4 0.0 copy-done.1
  89.4 1.9 %sub.3 = f32[512,4,256]{2,1,0:T(4,128)} subtract(f32[512,4,256]{2,1,0:T(4,128)S(1)} %copy-done.1, f32[512,4,256]{2,1,0:T(4,128)S(1)} %all_to_all.11) | non-fusion elementwise | flops 524288 | bytes 6291456 | tf_op jit(solution)/shard_map/sub | solution.py:142
Async XLA Ops:
  3.6 49.8 %copy-start = (f32[512,4,256]{2,1,0:T(4,128)}, f32[512,4,256]{2,1,0:T(4,128)S(1)}, u32[]{:S(2)}) copy-start(f32[512,4,256]{2,1,0:T(4,128)S(1)} %multiply_add_fusion) | copy-start | bytes 6291460
  53.4 36.0 %copy-start.1 = (f32[512,4,256]{2,1,0:T(4,128)S(1)}, f32[512,4,256]{2,1,0:T(4,128)}, u32[]{:S(2)}) copy-start(f32[512,4,256]{2,1,0:T(4,128)} %param.5) | copy-start | bytes 6291460

commit v4 on v3

--- a/solution.py
+++ b/solution.py
@@ -31,7 +31,7 @@
 
 
 def orthogonal(rows, cols, mats):
-    def body(in_ref, out_ref, x_ref):
+    def body(in_ref, kept_ref, out_ref, kept_out_ref, x_ref, written):
         here, wide = in_ref.shape[1], in_ref.shape[2]
         side = here * rows
         lane = lax.broadcasted_iota(jnp.int32, (side, 2 * side), 1)
@@ -95,6 +95,8 @@
         def pair_up(values):
             return [jnp.concatenate(values[m : m + 2], axis=1) for m in range(0, mats, 2)]
 
+        kept_copy = pltpu.make_async_copy(kept_ref, kept_out_ref, written)
+        kept_copy.start()
         for m in range(mats):
             for r in range(0, rows, 4):
                 for c in range(cols):
@@ -116,31 +118,101 @@
                 y = applied(weights, m, c * wide)
                 for r in range(rows):
                     out_ref[(r * cols + c) * mats + m] = y[r * here : (r + 1) * here]
-
-    def call(pieces):
+        kept_copy.wait()
+
+    def call(pieces, kept):
         n, here, wide = pieces.shape
         return pl.pallas_call(
             body,
-            out_shape=jax.ShapeDtypeStruct(pieces.shape, pieces.dtype),
-            in_specs=[pl.BlockSpec(memory_space=pltpu.VMEM)],
-            out_specs=pl.BlockSpec(memory_space=pltpu.VMEM),
-            scratch_shapes=[pltpu.VMEM((mats, 3 * here * rows, wide * cols), BF16)],
+            out_shape=(
+                jax.ShapeDtypeStruct(pieces.shape, pieces.dtype),
+                jax.ShapeDtypeStruct(kept.shape, kept.dtype),
+            ),
+            in_specs=[pl.BlockSpec(memory_space=pltpu.VMEM)] * 2,
+            out_specs=(pl.BlockSpec(memory_space=pltpu.VMEM), pl.BlockSpec(memory_space=pltpu.HBM)),
+            scratch_shapes=[
+                pltpu.VMEM((mats, 3 * here * rows, wide * cols), BF16),
+                pltpu.SemaphoreType.DMA,
+            ],
             compiler_params=pltpu.CompilerParams(vmem_limit_bytes=32 * 1024 * 1024),
             name="orthogonal",
-        )(pieces)
+        )(pieces, kept)
 
     return call
+
+
+PARTS = 8
+
+
+def fresh_momentum(grad_stack, moment_stack):
+    many = grad_stack.shape[0] // PARTS
+
+    def body(grad_ref, moment_ref, out_ref, grads, moments, arrived):
+        def copies(i):
+            part = pl.ds(i * many, many)
+            return (
+                pltpu.make_async_copy(grad_ref.at[part], grads.at[part], arrived.at[2 * i]),
+                pltpu.make_async_copy(moment_ref.at[part], moments.at[part], arrived.at[2 * i + 1]),
+            )
+
+        for i in range(PARTS):
+            for copy in copies(i):
+                copy.start()
+        for i in range(PARTS):
+            for copy in copies(i):
+                copy.wait()
+            part = pl.ds(i * many, many)
+            out_ref[part] = hold_rate * moments[part] + grads[part]
+
+    return pl.pallas_call(
+        body,
+        out_shape=pltpu.VMEM(grad_stack.shape, F32),
+        in_specs=[pl.BlockSpec(memory_space=pltpu.HBM)] * 2,
+        out_specs=pl.BlockSpec(memory_space=pltpu.VMEM),
+        scratch_shapes=[
+            pltpu.VMEM(grad_stack.shape, F32),
+            pltpu.VMEM(grad_stack.shape, F32),
+            pltpu.SemaphoreType.DMA((2 * PARTS,)),
+        ],
+        compiler_params=pltpu.CompilerParams(vmem_limit_bytes=61 * 1024 * 1024),
+        name="fresh_momentum",
+    )(grad_stack, moment_stack)
+
+
+def stepped(weight_stack, back):
+    many = back.shape[0] // PARTS
+
+    def body(weight_ref, back_ref, out_ref, made, sent):
+        def copy(i):
+            part = pl.ds(i * many, many)
+            return pltpu.make_async_copy(made.at[part], out_ref.at[part], sent.at[i])
+
+        for i in range(PARTS):
+            part = pl.ds(i * many, many)
+            made[part] = weight_ref[part] - learn_rate * back_ref[part]
+            copy(i).start()
+        for i in range(PARTS):
+            copy(i).wait()
+
+    return pl.pallas_call(
+        body,
+        out_shape=jax.ShapeDtypeStruct(back.shape, F32),
+        in_specs=[pl.BlockSpec(memory_space=pltpu.VMEM)] * 2,
+        out_specs=pl.BlockSpec(memory_space=pltpu.HBM),
+        scratch_shapes=[pltpu.VMEM(back.shape, F32), pltpu.SemaphoreType.DMA((PARTS,))],
+        compiler_params=pltpu.CompilerParams(vmem_limit_bytes=16 * 1024 * 1024),
+        name="stepped",
+    )(weight_stack, back)
 
 
 def on_device(grad_stack, moment_stack, weight_stack):
     axes = ("rows", "cols")
     rows, cols = lax.axis_size("rows"), lax.axis_size("cols")
-    new_momentum = hold_rate * moment_stack + grad_stack
+    new_momentum = fresh_momentum(grad_stack, moment_stack)
     pieces = lax.all_to_all(new_momentum, axes, split_axis=0, concat_axis=0, tiled=True)
-    pieces = orthogonal(rows, cols, pieces.shape[0] // (rows * cols))(pieces)
+    pieces, written = orthogonal(rows, cols, pieces.shape[0] // (rows * cols))(pieces, new_momentum)
     back = lax.all_to_all(pieces, axes, split_axis=0, concat_axis=0, tiled=True)
-    new_weights = weight_stack - learn_rate * back
-    return (new_weights, new_momentum)
+    return (stepped(weight_stack, back), written)
 
 
 def solution(mesh):

time: 91.4 us -> 90.3 us (0.988)
  other arithmetic: 4.8 us -> 0 us
  Pallas kernels: 6.9 us -> 10.6 us
    pallas_call x1 -> x3, Pallas kernels: 6.9 us -> 10.6 us  [the longest x1 6.92 us: call(): pl.pallas_call(body, out_shape=(jax.ShapeDtypeStruct(pieces.shape, pieces...]
    add x1 -> x0, other arithmetic: 2.94 us -> none  [on_device(): new_momentum = hold_rate * moment_stack + grad_stack]
    sub x1 -> x0, other arithmetic: 1.86 us -> none  [on_device(): new_weights = weight_stack - learn_rate * back]
where the time goes in v4:
time: 90.3 us; the launch traced here: 90.1 us
  blocking collectives  78.9 us (87%)
  Pallas kernels  10.6 us (12%)
    all_to_all x1, blocking collectives, on_device(): lax.all_to_all(new_momentum, axes, split_axis=0, concat_axis=0, tiled=True)  42.9 us
    all_to_all x1, blocking collectives, on_device(): back = lax.all_to_all(pieces, axes, split_axis=0, concat_axis=0, tiled=True)  36 us
    pallas_call x1, Pallas kernels, call(): pl.pallas_call(body, out_shape=(jax.ShapeDtypeStruct(pieces.shape, pieces...  6.92 us
    pallas_call x1, Pallas kernels, fresh_momentum(): pl.pallas_call(body, out_shape=pltpu.VMEM(grad_stack.shape, F32), in_spec...  2.31 us

profile of v4, /device:TPU:0, one launch (start us, length us, event | category | flops | bytes accessed | tf_op | source)
XLA Modules:
  0.0 90.1 jit_solution(14652500148950646313)
XLA Ops:
  0.6 2.3 %fresh_momentum.1.kept_ref = f32[512,4,256]{2,1,0:T(4,128)S(1)} custom-call(f32[512,4,256]{2,1,0:T(4,128)} %grad_ref.1, f32[512,4,256]{2,1,0:T(4,128)} %moment_ref.1), custom_call_target="tpu_custom_call" | custom-call | tf_op jit(solution)/shard_map/fresh_momentum/pallas_call | solution.py:167
  2.9 42.9 %all_to_all.10.in_ref = f32[512,4,256]{2,1,0:T(4,128)S(1)} all-to-all(f32[512,4,256]{2,1,0:T(4,128)S(1)} %fresh_momentum.1.kept_ref), channel_id=1, replica_groups=mesh['rows'=16,'cols'=8] {'rows','cols'}, dimensions={0} | all-to-all | bytes 4194304 | tf_op jit(solution)/shard_map/all_to_all | solution.py:212
  45.8 6.9 %orthogonal.1 = (f32[512,4,256]{2,1,0:T(4,128)S(1)}, f32[512,4,256]{2,1,0:T(4,128)}) custom-call(f32[512,4,256]{2,1,0:T(4,128)S(1)} %all_to_all.10.in_ref, f32[512,4,256]{2,1,0:T(4,128)S(1)} %fresh_momentum.1.kept_ref), custom_call_target="tpu_custom_call" | custom-call | tf_op jit(solution)/shard_map/orthogonal/pallas_call | solution.py:125
  52.7 0.0 copy-start
  52.8 36.0 %all_to_all.11.back_ref = f32[512,4,256]{2,1,0:T(4,128)S(1)} all-to-all(f32[512,4,256]{2,1,0:T(4,128)S(1)} %get-tuple-element.4), channel_id=1, replica_groups=mesh['rows'=16,'cols'=8] {'rows','cols'}, dimensions={0} | all-to-all | bytes 4194304 | tf_op jit(solution)/shard_map/all_to_all | solution.py:214
  88.7 0.0 copy-done
  88.7 1.4 %stepped.1 = f32[512,4,256]{2,1,0:T(4,128)} custom-call(f32[512,4,256]{2,1,0:T(4,128)S(1)} %copy-done, f32[512,4,256]{2,1,0:T(4,128)S(1)} %all_to_all.11.back_ref), custom_call_target="tpu_custom_call" | custom-call | tf_op jit(solution)/shard_map/stepped/pallas_call | solution.py:197
Async XLA Ops:
  52.7 36.0 %copy-start = (f32[512,4,256]{2,1,0:T(4,128)S(1)}, f32[512,4,256]{2,1,0:T(4,128)}, u32[]{:S(2)}) copy-start(f32[512,4,256]{2,1,0:T(4,128)} %weight_ref.1) | copy-start | bytes 6291460

commit v5 on v4

--- a/solution.py
+++ b/solution.py
@@ -37,7 +37,6 @@
         lane = lax.broadcasted_iota(jnp.int32, (side, 2 * side), 1)
         row = lax.broadcasted_iota(jnp.int32, (side, 2 * side), 0)
         eye = jnp.where((lane == row) | (lane == row + side), 1.0, 0.0).astype(F32)
-        eye_one = eye[:, :side]
         first = jnp.where(lane < side, 1.0, 0.0).astype(BF16)
         second = jnp.where(lane < side, 0.0, 1.0).astype(BF16)
 
@@ -45,10 +44,16 @@
             for k, term in enumerate(split3(value)):
                 x_ref[m, pl.ds(k * side + top, value.shape[0]), pl.ds(at, value.shape[1])] = term
 
-        def gram_of(m):
-            c = dot_t(x_ref[m, : 2 * side], x_ref[m])
-            half = c[:side, side : 2 * side] + (c[:side, 2 * side :] + 0.5 * c[side:, side : 2 * side])
-            return c[:side, :side] + (half + half.T)
+        def pair_gram(m):
+            def by_term(k, order):
+                terms = jnp.concatenate([x_ref[k, pl.ds(t * side, side)] for t in order], axis=0)
+                c = dot_t(x_ref[k], terms)
+                c = c[:side] + (c[side : 2 * side] + c[2 * side :])
+                tail = jnp.concatenate([c[:, 2 * side :], jnp.zeros((side, side), F32)], axis=1)
+                return c[:, : 2 * side] + tail
+
+            one, two = by_term(m, (0, 1, 2)), by_term(m + 1, (1, 0, 2))
+            return jnp.where(lane < side, one, two) + pltpu.roll(jnp.where(lane < side, two, one), side, 1)
 
         def streamed(value):
             v1, v2, v3 = split3(value)
@@ -58,17 +63,28 @@
             v1, v2, v3 = [jnp.concatenate([v * first, v * second], axis=0) for v in split3(value)]
             return jnp.concatenate([v1, v2, v3, v1, v2, v1], axis=0)
 
-        def steps(grams, lefts, count):
+        def steps(grams, count, normed):
             pairs = range(len(grams))
             for step in range(count):
                 gram_held = [held(g) for g in grams]
                 squares = [dot(streamed(grams[p]), gram_held[p]) for p in pairs]
-                polys = [3.4445 * eye - 4.775 * grams[p] + 2.0315 * squares[p] for p in pairs]
+                if step == 0 and normed:
+                    sizes = [norms(g) for g in grams]
+                    shrink = [1.0 / s for s in sizes]
+                    polys = [
+                        3.4445 * eye - (4.775 * shrink[p]) * grams[p] + (2.0315 * shrink[p]) * (shrink[p] * squares[p])
+                        for p in pairs
+                    ]
+                else:
+                    polys = [3.4445 * eye - 4.775 * grams[p] + 2.0315 * squares[p] for p in pairs]
                 flow = [streamed(poly) for poly in polys]
                 last = step + 1 == count
                 if step == 0:
                     mixed = None if last else [dot(flow[p], gram_held[p]) for p in pairs]
-                    lefts = [polys[p] if lefts is None else polys[p] * lefts[p] for p in pairs]
+                    lefts = polys
+                    if normed:
+                        lefts = [poly * lax.rsqrt(s) for poly, s in zip(polys, sizes)]
+                        mixed = None if last else [shrink[p] * mixed[p] for p in pairs]
                 elif last:
                     lefts = [dot(flow[p], held(lefts[p])) for p in pairs]
                 else:
@@ -79,21 +95,24 @@
                     grams = [dot(streamed(mixed[p]), held(polys[p])) for p in pairs]
             return lefts
 
+        def norms(gram):
+            diagonal = jnp.sum(gram * eye, axis=0, keepdims=True)
+            one = jnp.sum(jnp.where(lane[:1] < side, diagonal, 0.0), axis=1, keepdims=True)
+            two = jnp.sum(jnp.where(lane[:1] < side, 0.0, diagonal), axis=1, keepdims=True)
+            return jnp.where(lane[:1] < side, one, two) + 1e-06
+
         def weights_of(lefts, m):
-            left = lefts[m // 2][:, (m % 2) * side : (m % 2 + 1) * side]
-            q1, q2, q3 = split3(left)
-            none = jnp.zeros((side, 2 * side), BF16)
-            return jnp.concatenate(
-                [jnp.concatenate([q1, q1, q1, q2], axis=1), jnp.concatenate([q3, q2, none], axis=1)], axis=0
-            )
+            left = lefts[m // 2]
+            own = lane < side if m % 2 == 0 else lane >= side
+            q1, q2, q3 = split3(jnp.where(own, left, pltpu.roll(left, side, 1)))
+            after = jnp.concatenate([q2 * second + q1 * first, jnp.zeros_like(q1)], axis=0)
+            low = jnp.concatenate([q1, q3 * first + q2 * second], axis=0)
+            return jnp.concatenate([low, after], axis=1)
 
         def applied(weights, m, at):
             terms = x_ref[m, :, pl.ds(at, wide)]
             got = dot(weights, jnp.concatenate([terms, terms[:side]], axis=0))
             return got[:side] + got[side:]
-
-        def pair_up(values):
-            return [jnp.concatenate(values[m : m + 2], axis=1) for m in range(0, mats, 2)]
 
         kept_copy = pltpu.make_async_copy(kept_ref, kept_out_ref, written)
         kept_copy.start()
@@ -102,16 +121,12 @@
                 for c in range(cols):
                     piece = [in_ref[((r + k) * cols + c) * mats + m] for k in range(4)]
                     keep(m, r * here, c * wide, jnp.concatenate(piece, axis=0))
-        grams = [gram_of(m) for m in range(mats)]
-        sizes = [jnp.sum(g * eye_one, axis=(0, 1), keepdims=True) + 1e-06 for g in grams]
-        scales = [jnp.broadcast_to(lax.rsqrt(s), (side, side)) for s in sizes]
-        grams = [g / s for g, s in zip(grams, sizes)]
-        lefts = steps(pair_up(grams), pair_up(scales), RESTART)
+        lefts = steps([pair_gram(m) for m in range(0, mats, 2)], RESTART, True)
         for m in range(mats):
             weights = weights_of(lefts, m)
             for c in range(cols):
                 keep(m, 0, c * wide, applied(weights, m, c * wide))
-        lefts = steps(pair_up([gram_of(m) for m in range(mats)]), None, ITERS - RESTART)
+        lefts = steps([pair_gram(m) for m in range(0, mats, 2)], ITERS - RESTART, False)
         for m in range(mats):
             weights = weights_of(lefts, m)
             for c in range(cols):

time: 90.3 us -> 88.9 us (0.984)
  Pallas kernels: 10.6 us -> 9.18 us
    pallas_call x1, Pallas kernels: 6.92 us -> 5.48 us  [call(): pl.pallas_call(body, out_shape=(jax.ShapeDtypeStruct(pieces.shape, pieces...]
where the time goes in v5:
time: 88.9 us; the launch traced here: 88.7 us
  blocking collectives  78.9 us (89%)
  Pallas kernels  9.18 us (10%)
    all_to_all x1, blocking collectives, on_device(): lax.all_to_all(new_momentum, axes, split_axis=0, concat_axis=0, tiled=True)  42.9 us
    all_to_all x1, blocking collectives, on_device(): back = lax.all_to_all(pieces, axes, split_axis=0, concat_axis=0, tiled=True)  36 us
    pallas_call x1, Pallas kernels, call(): pl.pallas_call(body, out_shape=(jax.ShapeDtypeStruct(pieces.shape, pieces...  5.48 us
    pallas_call x1, Pallas kernels, fresh_momentum(): pl.pallas_call(body, out_shape=pltpu.VMEM(grad_stack.shape, F32), in_spec...  2.31 us

profile of v5, /device:TPU:0, one launch (start us, length us, event | category | flops | bytes accessed | tf_op | source)
XLA Modules:
  0.0 88.7 jit_solution(2948999374059762009)
XLA Ops:
  0.6 2.3 %fresh_momentum.1.kept_ref = f32[512,4,256]{2,1,0:T(4,128)S(1)} custom-call(f32[512,4,256]{2,1,0:T(4,128)} %grad_ref.1, f32[512,4,256]{2,1,0:T(4,128)} %moment_ref.1), custom_call_target="tpu_custom_call" | custom-call | tf_op jit(solution)/shard_map/fresh_momentum/pallas_call | solution.py:182
  2.9 42.9 %all_to_all.10.in_ref = f32[512,4,256]{2,1,0:T(4,128)S(1)} all-to-all(f32[512,4,256]{2,1,0:T(4,128)S(1)} %fresh_momentum.1.kept_ref), channel_id=1, replica_groups=mesh['rows'=16,'cols'=8] {'rows','cols'}, dimensions={0} | all-to-all | bytes 4194304 | tf_op jit(solution)/shard_map/all_to_all | solution.py:227
  45.8 5.5 %orthogonal.1 = (f32[512,4,256]{2,1,0:T(4,128)S(1)}, f32[512,4,256]{2,1,0:T(4,128)}) custom-call(f32[512,4,256]{2,1,0:T(4,128)S(1)} %all_to_all.10.in_ref, f32[512,4,256]{2,1,0:T(4,128)S(1)} %fresh_momentum.1.kept_ref), custom_call_target="tpu_custom_call" | custom-call | tf_op jit(solution)/shard_map/orthogonal/pallas_call | solution.py:140
  51.3 0.0 copy-start
  51.3 36.0 %all_to_all.11.back_ref = f32[512,4,256]{2,1,0:T(4,128)S(1)} all-to-all(f32[512,4,256]{2,1,0:T(4,128)S(1)} %get-tuple-element.4), channel_id=1, replica_groups=mesh['rows'=16,'cols'=8] {'rows','cols'}, dimensions={0} | all-to-all | bytes 4194304 | tf_op jit(solution)/shard_map/all_to_all | solution.py:229
  87.3 0.0 copy-done
  87.3 1.4 %stepped.1 = f32[512,4,256]{2,1,0:T(4,128)} custom-call(f32[512,4,256]{2,1,0:T(4,128)S(1)} %copy-done, f32[512,4,256]{2,1,0:T(4,128)S(1)} %all_to_all.11.back_ref), custom_call_target="tpu_custom_call" | custom-call | tf_op jit(solution)/shard_map/stepped/pallas_call | solution.py:212
Async XLA Ops:
  51.3 36.0 %copy-start = (f32[512,4,256]{2,1,0:T(4,128)S(1)}, f32[512,4,256]{2,1,0:T(4,128)}, u32[]{:S(2)}) copy-start(f32[512,4,256]{2,1,0:T(4,128)} %weight_ref.1) | copy-start | bytes 6291460

commit v6 on v5

--- a/solution.py
+++ b/solution.py
@@ -40,34 +40,41 @@
         first = jnp.where(lane < side, 1.0, 0.0).astype(BF16)
         second = jnp.where(lane < side, 0.0, 1.0).astype(BF16)
 
-        def keep(m, top, at, value):
-            for k, term in enumerate(split3(value)):
+        def keep(m, top, at, value, terms):
+            for k, term in enumerate(split3(value)[:terms]):
                 x_ref[m, pl.ds(k * side + top, value.shape[0]), pl.ds(at, value.shape[1])] = term
 
-        def pair_gram(m):
+        def pair_gram(m, terms):
             def by_term(k, order):
-                terms = jnp.concatenate([x_ref[k, pl.ds(t * side, side)] for t in order], axis=0)
-                c = dot_t(x_ref[k], terms)
+                held_terms = jnp.concatenate([x_ref[k, pl.ds(t * side, side)] for t in order], axis=0)
+                c = dot_t(x_ref[k, : terms * side], held_terms)
+                if terms == 2:
+                    return c[:side] + c[side:]
                 c = c[:side] + (c[side : 2 * side] + c[2 * side :])
                 tail = jnp.concatenate([c[:, 2 * side :], jnp.zeros((side, side), F32)], axis=1)
                 return c[:, : 2 * side] + tail
 
-            one, two = by_term(m, (0, 1, 2)), by_term(m + 1, (1, 0, 2))
+            one, two = by_term(m, (0, 1, 2)[:terms]), by_term(m + 1, (1, 0, 2)[:terms])
             return jnp.where(lane < side, one, two) + pltpu.roll(jnp.where(lane < side, two, one), side, 1)
 
         def streamed(value):
             v1, v2, v3 = split3(value)
-            return jnp.concatenate([v1, v1, v1, v2, v2, v3], axis=1)
+            return jnp.concatenate([v1, v2, v3, v1], axis=1)
 
         def held(value):
             v1, v2, v3 = [jnp.concatenate([v * first, v * second], axis=0) for v in split3(value)]
-            return jnp.concatenate([v1, v2, v3, v1, v2, v1], axis=0)
+            high = jnp.concatenate([v1, v2], axis=1)
+            return jnp.concatenate([high, high], axis=0), jnp.concatenate([v1, v3], axis=0)
+
+        def product(flow, weights):
+            high = dot(flow[:, : 4 * side], weights[0])
+            return high[:, : 2 * side] + (high[:, 2 * side :] + dot(flow[:, 4 * side :], weights[1]))
 
         def steps(grams, count, normed):
             pairs = range(len(grams))
             for step in range(count):
                 gram_held = [held(g) for g in grams]
-                squares = [dot(streamed(grams[p]), gram_held[p]) for p in pairs]
+                squares = [product(streamed(grams[p]), gram_held[p]) for p in pairs]
                 if step == 0 and normed:
                     sizes = [norms(g) for g in grams]
                     shrink = [1.0 / s for s in sizes]
@@ -80,19 +87,18 @@
                 flow = [streamed(poly) for poly in polys]
                 last = step + 1 == count
                 if step == 0:
-                    mixed = None if last else [dot(flow[p], gram_held[p]) for p in pairs]
+                    mixed = None if last else [product(flow[p], gram_held[p]) for p in pairs]
                     lefts = polys
                     if normed:
                         lefts = [poly * lax.rsqrt(s) for poly, s in zip(polys, sizes)]
                         mixed = None if last else [shrink[p] * mixed[p] for p in pairs]
                 elif last:
-                    lefts = [dot(flow[p], held(lefts[p])) for p in pairs]
+                    lefts = [product(flow[p], held(lefts[p])) for p in pairs]
                 else:
-                    both = [dot(flow[p], jnp.concatenate([held(lefts[p]), gram_held[p]], axis=1)) for p in pairs]
-                    lefts = [b[:, : 2 * side] for b in both]
-                    mixed = [b[:, 2 * side :] for b in both]
+                    mixed = [product(flow[p], gram_held[p]) for p in pairs]
+                    lefts = [product(flow[p], held(lefts[p])) for p in pairs]
                 if not last:
-                    grams = [dot(streamed(mixed[p]), held(polys[p])) for p in pairs]
+                    grams = [product(streamed(mixed[p]), held(polys[p])) for p in pairs]
             return lefts
 
         def norms(gram):
@@ -101,18 +107,20 @@
             two = jnp.sum(jnp.where(lane[:1] < side, 0.0, diagonal), axis=1, keepdims=True)
             return jnp.where(lane[:1] < side, one, two) + 1e-06
 
-        def weights_of(lefts, m):
+        def weights_of(lefts, m, terms):
             left = lefts[m // 2]
             own = lane < side if m % 2 == 0 else lane >= side
             q1, q2, q3 = split3(jnp.where(own, left, pltpu.roll(left, side, 1)))
-            after = jnp.concatenate([q2 * second + q1 * first, jnp.zeros_like(q1)], axis=0)
-            low = jnp.concatenate([q1, q3 * first + q2 * second], axis=0)
-            return jnp.concatenate([low, after], axis=1)
-
-        def applied(weights, m, at):
-            terms = x_ref[m, :, pl.ds(at, wide)]
-            got = dot(weights, jnp.concatenate([terms, terms[:side]], axis=0))
-            return got[:side] + got[side:]
+            if terms == 2:
+                return jnp.concatenate([q1, q2 * first + q3 * second], axis=1)
+            high = jnp.concatenate([q1, q1 * first + q2 * second], axis=1)
+            rest = jnp.concatenate([q3 * first + q2 * second, jnp.zeros_like(q1)], axis=1)
+            return jnp.concatenate([high, rest], axis=0)
+
+        def applied(weights, m, at, terms):
+            rows_of = x_ref[m, : terms * side, pl.ds(at, wide)]
+            got = dot(weights, jnp.concatenate([rows_of] + [rows_of[:side]] * (4 - terms), axis=0))
+            return got if terms == 2 else got[:side] + got[side:]
 
         kept_copy = pltpu.make_async_copy(kept_ref, kept_out_ref, written)
         kept_copy.start()
@@ -120,17 +128,17 @@
             for r in range(0, rows, 4):
                 for c in range(cols):
                     piece = [in_ref[((r + k) * cols + c) * mats + m] for k in range(4)]
-                    keep(m, r * here, c * wide, jnp.concatenate(piece, axis=0))
-        lefts = steps([pair_gram(m) for m in range(0, mats, 2)], RESTART, True)
+                    keep(m, r * here, c * wide, jnp.concatenate(piece, axis=0), 3)
+        lefts = steps([pair_gram(m, 3) for m in range(0, mats, 2)], RESTART, True)
         for m in range(mats):
-            weights = weights_of(lefts, m)
+            weights = weights_of(lefts, m, 3)
             for c in range(cols):
-                keep(m, 0, c * wide, applied(weights, m, c * wide))
-        lefts = steps([pair_gram(m) for m in range(0, mats, 2)], ITERS - RESTART, False)
+                keep(m, 0, c * wide, applied(weights, m, c * wide, 3), 2)
+        lefts = steps([pair_gram(m, 2) for m in range(0, mats, 2)], ITERS - RESTART, False)
         for m in range(mats):
-            weights = weights_of(lefts, m)
+            weights = weights_of(lefts, m, 2)
             for c in range(cols):
-                y = applied(weights, m, c * wide)
+                y = applied(weights, m, c * wide, 2)
                 for r in range(rows):
                     out_ref[(r * cols + c) * mats + m] = y[r * here : (r + 1) * here]
         kept_copy.wait()

time: 88.9 us -> 88.5 us (level)
  no operation moved by 1% of the time
where the time goes in v6:
time: 88.5 us; the launch traced here: 88.4 us
  blocking collectives  78.9 us (89%)
  Pallas kernels  8.87 us (10%)
    all_to_all x1, blocking collectives, on_device(): lax.all_to_all(new_momentum, axes, split_axis=0, concat_axis=0, tiled=True)  42.9 us
    all_to_all x1, blocking collectives, on_device(): back = lax.all_to_all(pieces, axes, split_axis=0, concat_axis=0, tiled=True)  36 us
    pallas_call x1, Pallas kernels, call(): pl.pallas_call(body, out_shape=(jax.ShapeDtypeStruct(pieces.shape, pieces...  5.16 us
    pallas_call x1, Pallas kernels, fresh_momentum(): pl.pallas_call(body, out_shape=pltpu.VMEM(grad_stack.shape, F32), in_spec...  2.31 us

profile of v6, /device:TPU:0, one launch (start us, length us, event | category | flops | bytes accessed | tf_op | source)
XLA Modules:
  0.0 88.4 jit_solution(8787609065293968943)
XLA Ops:
  0.6 2.3 %fresh_momentum.1.kept_ref = f32[512,4,256]{2,1,0:T(4,128)S(1)} custom-call(f32[512,4,256]{2,1,0:T(4,128)} %grad_ref.1, f32[512,4,256]{2,1,0:T(4,128)} %moment_ref.1), custom_call_target="tpu_custom_call" | custom-call | tf_op jit(solution)/shard_map/fresh_momentum/pallas_call | solution.py:190
  2.9 42.9 %all_to_all.10.in_ref = f32[512,4,256]{2,1,0:T(4,128)S(1)} all-to-all(f32[512,4,256]{2,1,0:T(4,128)S(1)} %fresh_momentum.1.kept_ref), channel_id=1, replica_groups=mesh['rows'=16,'cols'=8] {'rows','cols'}, dimensions={0} | all-to-all | bytes 4194304 | tf_op jit(solution)/shard_map/all_to_all | solution.py:235
  45.8 5.2 %orthogonal.1 = (f32[512,4,256]{2,1,0:T(4,128)S(1)}, f32[512,4,256]{2,1,0:T(4,128)}) custom-call(f32[512,4,256]{2,1,0:T(4,128)S(1)} %all_to_all.10.in_ref, f32[512,4,256]{2,1,0:T(4,128)S(1)} %fresh_momentum.1.kept_ref), custom_call_target="tpu_custom_call" | custom-call | tf_op jit(solution)/shard_map/orthogonal/pallas_call | solution.py:148
  51.0 0.0 copy-start
  51.0 36.0 %all_to_all.11.back_ref = f32[512,4,256]{2,1,0:T(4,128)S(1)} all-to-all(f32[512,4,256]{2,1,0:T(4,128)S(1)} %get-tuple-element.4), channel_id=1, replica_groups=mesh['rows'=16,'cols'=8] {'rows','cols'}, dimensions={0} | all-to-all | bytes 4194304 | tf_op jit(solution)/shard_map/all_to_all | solution.py:237
  87.0 0.0 copy-done
  87.0 1.4 %stepped.1 = f32[512,4,256]{2,1,0:T(4,128)} custom-call(f32[512,4,256]{2,1,0:T(4,128)S(1)} %copy-done, f32[512,4,256]{2,1,0:T(4,128)S(1)} %all_to_all.11.back_ref), custom_call_target="tpu_custom_call" | custom-call | tf_op jit(solution)/shard_map/stepped/pallas_call | solution.py:220
Async XLA Ops:
  51.0 36.0 %copy-start = (f32[512,4,256]{2,1,0:T(4,128)S(1)}, f32[512,4,256]{2,1,0:T(4,128)}, u32[]{:S(2)}) copy-start(f32[512,4,256]{2,1,0:T(4,128)} %weight_ref.1) | copy-start | bytes 6291460

commit v7 on v6

--- a/solution.py
+++ b/solution.py
@@ -57,24 +57,28 @@
             one, two = by_term(m, (0, 1, 2)[:terms]), by_term(m + 1, (1, 0, 2)[:terms])
             return jnp.where(lane < side, one, two) + pltpu.roll(jnp.where(lane < side, two, one), side, 1)
 
-        def streamed(value):
-            v1, v2, v3 = split3(value)
-            return jnp.concatenate([v1, v2, v3, v1], axis=1)
-
-        def held(value):
-            v1, v2, v3 = [jnp.concatenate([v * first, v * second], axis=0) for v in split3(value)]
-            high = jnp.concatenate([v1, v2], axis=1)
-            return jnp.concatenate([high, high], axis=0), jnp.concatenate([v1, v3], axis=0)
+        def streamed(value, terms):
+            v = split3(value)
+            return jnp.concatenate(v[:2] if terms == 2 else [v[0], v[1], v[2], v[0]], axis=1)
+
+        def held(value, terms):
+            v = [jnp.concatenate([v * first, v * second], axis=0) for v in split3(value)[:terms]]
+            high = jnp.concatenate(v[:2], axis=1)
+            high = jnp.concatenate([high, high], axis=0)
+            return (high,) if terms == 2 else (high, jnp.concatenate([v[0], v[2]], axis=0))
 
         def product(flow, weights):
             high = dot(flow[:, : 4 * side], weights[0])
-            return high[:, : 2 * side] + (high[:, 2 * side :] + dot(flow[:, 4 * side :], weights[1]))
-
-        def steps(grams, count, normed):
+            low = high[:, 2 * side :]
+            if len(weights) == 2:
+                low = low + dot(flow[:, 4 * side :], weights[1])
+            return high[:, : 2 * side] + low
+
+        def steps(grams, count, normed, terms):
             pairs = range(len(grams))
             for step in range(count):
-                gram_held = [held(g) for g in grams]
-                squares = [product(streamed(grams[p]), gram_held[p]) for p in pairs]
+                gram_held = [held(g, terms) for g in grams]
+                squares = [product(streamed(grams[p], terms), gram_held[p]) for p in pairs]
                 if step == 0 and normed:
                     sizes = [norms(g) for g in grams]
                     shrink = [1.0 / s for s in sizes]
@@ -84,7 +88,7 @@
                     ]
                 else:
                     polys = [3.4445 * eye - 4.775 * grams[p] + 2.0315 * squares[p] for p in pairs]
-                flow = [streamed(poly) for poly in polys]
+                flow = [streamed(poly, terms) for poly in polys]
                 last = step + 1 == count
                 if step == 0:
                     mixed = None if last else [product(flow[p], gram_held[p]) for p in pairs]
@@ -93,12 +97,12 @@
                         lefts = [poly * lax.rsqrt(s) for poly, s in zip(polys, sizes)]
                         mixed = None if last else [shrink[p] * mixed[p] for p in pairs]
                 elif last:
-                    lefts = [product(flow[p], held(lefts[p])) for p in pairs]
+                    lefts = [product(flow[p], held(lefts[p], terms)) for p in pairs]
                 else:
                     mixed = [product(flow[p], gram_held[p]) for p in pairs]
-                    lefts = [product(flow[p], held(lefts[p])) for p in pairs]
+                    lefts = [product(flow[p], held(lefts[p], terms)) for p in pairs]
                 if not last:
-                    grams = [product(streamed(mixed[p]), held(polys[p])) for p in pairs]
+                    grams = [product(streamed(mixed[p], terms), held(polys[p], terms)) for p in pairs]
             return lefts
 
         def norms(gram):
@@ -129,12 +133,12 @@
                 for c in range(cols):
                     piece = [in_ref[((r + k) * cols + c) * mats + m] for k in range(4)]
                     keep(m, r * here, c * wide, jnp.concatenate(piece, axis=0), 3)
-        lefts = steps([pair_gram(m, 3) for m in range(0, mats, 2)], RESTART, True)
+        lefts = steps([pair_gram(m, 3) for m in range(0, mats, 2)], RESTART, True, 3)
         for m in range(mats):
             weights = weights_of(lefts, m, 3)
             for c in range(cols):
                 keep(m, 0, c * wide, applied(weights, m, c * wide, 3), 2)
-        lefts = steps([pair_gram(m, 2) for m in range(0, mats, 2)], ITERS - RESTART, False)
+        lefts = steps([pair_gram(m, 2) for m in range(0, mats, 2)], ITERS - RESTART, False, 2)
         for m in range(mats):
             weights = weights_of(lefts, m, 2)
             for c in range(cols):

time: 88.5 us -> 88.2 us (level)
  no operation moved by 1% of the time
where the time goes in v7:
time: 88.2 us; the launch traced here: 88.1 us
  blocking collectives  78.9 us (89%)
  Pallas kernels  8.54 us (10%)
    all_to_all x1, blocking collectives, on_device(): lax.all_to_all(new_momentum, axes, split_axis=0, concat_axis=0, tiled=True)  42.9 us
    all_to_all x1, blocking collectives, on_device(): back = lax.all_to_all(pieces, axes, split_axis=0, concat_axis=0, tiled=True)  36 us
    pallas_call x1, Pallas kernels, call(): pl.pallas_call(body, out_shape=(jax.ShapeDtypeStruct(pieces.shape, pieces...  4.83 us
    pallas_call x1, Pallas kernels, fresh_momentum(): pl.pallas_call(body, out_shape=pltpu.VMEM(grad_stack.shape, F32), in_spec...  2.31 us

profile of v7, /device:TPU:0, one launch (start us, length us, event | category | flops | bytes accessed | tf_op | source)
XLA Modules:
  0.0 88.1 jit_solution(3581519235896121256)
XLA Ops:
  0.6 2.3 %fresh_momentum.1.kept_ref = f32[512,4,256]{2,1,0:T(4,128)S(1)} custom-call(f32[512,4,256]{2,1,0:T(4,128)} %grad_ref.1, f32[512,4,256]{2,1,0:T(4,128)} %moment_ref.1), custom_call_target="tpu_custom_call" | custom-call | tf_op jit(solution)/shard_map/fresh_momentum/pallas_call | solution.py:194
  2.9 42.9 %all_to_all.10.in_ref = f32[512,4,256]{2,1,0:T(4,128)S(1)} all-to-all(f32[512,4,256]{2,1,0:T(4,128)S(1)} %fresh_momentum.1.kept_ref), channel_id=1, replica_groups=mesh['rows'=16,'cols'=8] {'rows','cols'}, dimensions={0} | all-to-all | bytes 4194304 | tf_op jit(solution)/shard_map/all_to_all | solution.py:239
  45.8 4.8 %orthogonal.1 = (f32[512,4,256]{2,1,0:T(4,128)S(1)}, f32[512,4,256]{2,1,0:T(4,128)}) custom-call(f32[512,4,256]{2,1,0:T(4,128)S(1)} %all_to_all.10.in_ref, f32[512,4,256]{2,1,0:T(4,128)S(1)} %fresh_momentum.1.kept_ref), custom_call_target="tpu_custom_call" | custom-call | tf_op jit(solution)/shard_map/orthogonal/pallas_call | solution.py:152
  50.7 0.0 copy-start
  50.7 36.0 %all_to_all.11.back_ref = f32[512,4,256]{2,1,0:T(4,128)S(1)} all-to-all(f32[512,4,256]{2,1,0:T(4,128)S(1)} %get-tuple-element.4), channel_id=1, replica_groups=mesh['rows'=16,'cols'=8] {'rows','cols'}, dimensions={0} | all-to-all | bytes 4194304 | tf_op jit(solution)/shard_map/all_to_all | solution.py:241
  86.7 0.0 copy-done
  86.7 1.4 %stepped.1 = f32[512,4,256]{2,1,0:T(4,128)} custom-call(f32[512,4,256]{2,1,0:T(4,128)S(1)} %copy-done, f32[512,4,256]{2,1,0:T(4,128)S(1)} %all_to_all.11.back_ref), custom_call_target="tpu_custom_call" | custom-call | tf_op jit(solution)/shard_map/stepped/pallas_call | solution.py:224
Async XLA Ops:
  50.7 36.0 %copy-start = (f32[512,4,256]{2,1,0:T(4,128)S(1)}, f32[512,4,256]{2,1,0:T(4,128)}, u32[]{:S(2)}) copy-start(f32[512,4,256]{2,1,0:T(4,128)} %weight_ref.1) | copy-start | bytes 6291460

commit v8 on v7

--- a/solution.py
+++ b/solution.py
@@ -65,14 +65,14 @@
             v = [jnp.concatenate([v * first, v * second], axis=0) for v in split3(value)[:terms]]
             high = jnp.concatenate(v[:2], axis=1)
             high = jnp.concatenate([high, high], axis=0)
-            return (high,) if terms == 2 else (high, jnp.concatenate([v[0], v[2]], axis=0))
+            if terms == 3:
+                tail = jnp.concatenate([v[0], v[2]], axis=0)
+                high = jnp.concatenate([high, jnp.concatenate([tail, jnp.zeros_like(tail)], axis=1)], axis=0)
+            return high
 
         def product(flow, weights):
-            high = dot(flow[:, : 4 * side], weights[0])
-            low = high[:, 2 * side :]
-            if len(weights) == 2:
-                low = low + dot(flow[:, 4 * side :], weights[1])
-            return high[:, : 2 * side] + low
+            got = dot(flow, weights)
+            return got[:, : 2 * side] + got[:, 2 * side :]
 
         def steps(grams, count, normed, terms):
             pairs = range(len(grams))

time: 88.2 us -> 88.2 us (level)
  no operation moved by 1% of the time
where the time goes in v8:
time: 88.2 us; the launch traced here: 88.1 us
  blocking collectives  78.9 us (89%)
  Pallas kernels  8.54 us (10%)
    all_to_all x1, blocking collectives, on_device(): lax.all_to_all(new_momentum, axes, split_axis=0, concat_axis=0, tiled=True)  42.9 us
    all_to_all x1, blocking collectives, on_device(): back = lax.all_to_all(pieces, axes, split_axis=0, concat_axis=0, tiled=True)  36 us
    pallas_call x1, Pallas kernels, call(): pl.pallas_call(body, out_shape=(jax.ShapeDtypeStruct(pieces.shape, pieces...  4.83 us
    pallas_call x1, Pallas kernels, fresh_momentum(): pl.pallas_call(body, out_shape=pltpu.VMEM(grad_stack.shape, F32), in_spec...  2.31 us

profile of v8, /device:TPU:0, one launch (start us, length us, event | category | flops | bytes accessed | tf_op | source)
XLA Modules:
  0.0 88.1 jit_solution(5971852519928406418)
XLA Ops:
  0.6 2.3 %fresh_momentum.1.kept_ref = f32[512,4,256]{2,1,0:T(4,128)S(1)} custom-call(f32[512,4,256]{2,1,0:T(4,128)} %grad_ref.1, f32[512,4,256]{2,1,0:T(4,128)} %moment_ref.1), custom_call_target="tpu_custom_call" | custom-call | tf_op jit(solution)/shard_map/fresh_momentum/pallas_call | solution.py:194
  2.9 42.9 %all_to_all.10.in_ref = f32[512,4,256]{2,1,0:T(4,128)S(1)} all-to-all(f32[512,4,256]{2,1,0:T(4,128)S(1)} %fresh_momentum.1.kept_ref), channel_id=1, replica_groups=mesh['rows'=16,'cols'=8] {'rows','cols'}, dimensions={0} | all-to-all | bytes 4194304 | tf_op jit(solution)/shard_map/all_to_all | solution.py:239
  45.8 4.8 %orthogonal.1 = (f32[512,4,256]{2,1,0:T(4,128)S(1)}, f32[512,4,256]{2,1,0:T(4,128)}) custom-call(f32[512,4,256]{2,1,0:T(4,128)S(1)} %all_to_all.10.in_ref, f32[512,4,256]{2,1,0:T(4,128)S(1)} %fresh_momentum.1.kept_ref), custom_call_target="tpu_custom_call" | custom-call | tf_op jit(solution)/shard_map/orthogonal/pallas_call | solution.py:152
  50.6 0.0 copy-start
  50.7 36.0 %all_to_all.11.back_ref = f32[512,4,256]{2,1,0:T(4,128)S(1)} all-to-all(f32[512,4,256]{2,1,0:T(4,128)S(1)} %get-tuple-element.4), channel_id=1, replica_groups=mesh['rows'=16,'cols'=8] {'rows','cols'}, dimensions={0} | all-to-all | bytes 4194304 | tf_op jit(solution)/shard_map/all_to_all | solution.py:241
  86.6 0.0 copy-done
  86.6 1.4 %stepped.1 = f32[512,4,256]{2,1,0:T(4,128)} custom-call(f32[512,4,256]{2,1,0:T(4,128)S(1)} %copy-done, f32[512,4,256]{2,1,0:T(4,128)S(1)} %all_to_all.11.back_ref), custom_call_target="tpu_custom_call" | custom-call | tf_op jit(solution)/shard_map/stepped/pallas_call | solution.py:224
Async XLA Ops:
  50.6 36.0 %copy-start = (f32[512,4,256]{2,1,0:T(4,128)S(1)}, f32[512,4,256]{2,1,0:T(4,128)}, u32[]{:S(2)}) copy-start(f32[512,4,256]{2,1,0:T(4,128)} %weight_ref.1) | copy-start | bytes 6291460

commit v9 on v7

--- a/solution.py
+++ b/solution.py
@@ -31,7 +31,8 @@
 
 
 def orthogonal(rows, cols, mats):
-    def body(in_ref, kept_ref, out_ref, kept_out_ref, x_ref, written):
+    def body(in_ref, kept_ref, out_ref, kept_out_ref, *scratch):
+        x_refs, written = scratch[:-1], scratch[-1]
         here, wide = in_ref.shape[1], in_ref.shape[2]
         side = here * rows
         lane = lax.broadcasted_iota(jnp.int32, (side, 2 * side), 1)
@@ -42,12 +43,12 @@
 
         def keep(m, top, at, value, terms):
             for k, term in enumerate(split3(value)[:terms]):
-                x_ref[m, pl.ds(k * side + top, value.shape[0]), pl.ds(at, value.shape[1])] = term
+                x_refs[m][pl.ds(k * side + top, value.shape[0]), pl.ds(at, value.shape[1])] = term
 
         def pair_gram(m, terms):
             def by_term(k, order):
-                held_terms = jnp.concatenate([x_ref[k, pl.ds(t * side, side)] for t in order], axis=0)
-                c = dot_t(x_ref[k, : terms * side], held_terms)
+                held_terms = jnp.concatenate([x_refs[k][pl.ds(t * side, side)] for t in order], axis=0)
+                c = dot_t(x_refs[k][: terms * side], held_terms)
                 if terms == 2:
                     return c[:side] + c[side:]
                 c = c[:side] + (c[side : 2 * side] + c[2 * side :])
@@ -74,36 +75,33 @@
                 low = low + dot(flow[:, 4 * side :], weights[1])
             return high[:, : 2 * side] + low
 
-        def steps(grams, count, normed, terms):
-            pairs = range(len(grams))
+        def steps(gram, count, normed, terms, box):
             for step in range(count):
-                gram_held = [held(g, terms) for g in grams]
-                squares = [product(streamed(grams[p], terms), gram_held[p]) for p in pairs]
+                gram_held = held(gram, terms)
+                square = product(streamed(gram, terms), gram_held)
                 if step == 0 and normed:
-                    sizes = [norms(g) for g in grams]
-                    shrink = [1.0 / s for s in sizes]
-                    polys = [
-                        3.4445 * eye - (4.775 * shrink[p]) * grams[p] + (2.0315 * shrink[p]) * (shrink[p] * squares[p])
-                        for p in pairs
-                    ]
+                    size = norms(gram)
+                    shrink = 1.0 / size
+                yield
+                if step == 0 and normed:
+                    poly = 3.4445 * eye - (4.775 * shrink) * gram + (2.0315 * shrink) * (shrink * square)
                 else:
-                    polys = [3.4445 * eye - 4.775 * grams[p] + 2.0315 * squares[p] for p in pairs]
-                flow = [streamed(poly, terms) for poly in polys]
+                    poly = 3.4445 * eye - 4.775 * gram + 2.0315 * square
+                flow = streamed(poly, terms)
                 last = step + 1 == count
+                if not last:
+                    mixed = product(flow, gram_held)
+                    if step == 0 and normed:
+                        mixed = shrink * mixed
                 if step == 0:
-                    mixed = None if last else [product(flow[p], gram_held[p]) for p in pairs]
-                    lefts = polys
-                    if normed:
-                        lefts = [poly * lax.rsqrt(s) for poly, s in zip(polys, sizes)]
-                        mixed = None if last else [shrink[p] * mixed[p] for p in pairs]
-                elif last:
-                    lefts = [product(flow[p], held(lefts[p], terms)) for p in pairs]
+                    left = poly * lax.rsqrt(size) if normed else poly
                 else:
-                    mixed = [product(flow[p], gram_held[p]) for p in pairs]
-                    lefts = [product(flow[p], held(lefts[p], terms)) for p in pairs]
+                    left = product(flow, held(left, terms))
+                yield
                 if not last:
-                    grams = [product(streamed(mixed[p], terms), held(polys[p], terms)) for p in pairs]
-            return lefts
+                    gram = product(streamed(mixed, terms), held(poly, terms))
+                    yield
+            box.append(left)
 
         def norms(gram):
             diagonal = jnp.sum(gram * eye, axis=0, keepdims=True)
@@ -111,8 +109,7 @@
             two = jnp.sum(jnp.where(lane[:1] < side, 0.0, diagonal), axis=1, keepdims=True)
             return jnp.where(lane[:1] < side, one, two) + 1e-06
 
-        def weights_of(lefts, m, terms):
-            left = lefts[m // 2]
+        def weights_of(left, m, terms):
             own = lane < side if m % 2 == 0 else lane >= side
             q1, q2, q3 = split3(jnp.where(own, left, pltpu.roll(left, side, 1)))
             if terms == 2:
@@ -122,29 +119,41 @@
             return jnp.concatenate([high, rest], axis=0)
 
         def applied(weights, m, at, terms):
-            rows_of = x_ref[m, : terms * side, pl.ds(at, wide)]
+            rows_of = x_refs[m][: terms * side, pl.ds(at, wide)]
             got = dot(weights, jnp.concatenate([rows_of] + [rows_of[:side]] * (4 - terms), axis=0))
             return got if terms == 2 else got[:side] + got[side:]
 
         kept_copy = pltpu.make_async_copy(kept_ref, kept_out_ref, written)
         kept_copy.start()
-        for m in range(mats):
-            for r in range(0, rows, 4):
-                for c in range(cols):
-                    piece = [in_ref[((r + k) * cols + c) * mats + m] for k in range(4)]
-                    keep(m, r * here, c * wide, jnp.concatenate(piece, axis=0), 3)
-        lefts = steps([pair_gram(m, 3) for m in range(0, mats, 2)], RESTART, True, 3)
-        for m in range(mats):
-            weights = weights_of(lefts, m, 3)
+        def pair(p):
+            both, box = (2 * p, 2 * p + 1), []
             for c in range(cols):
-                keep(m, 0, c * wide, applied(weights, m, c * wide, 3), 2)
-        lefts = steps([pair_gram(m, 2) for m in range(0, mats, 2)], ITERS - RESTART, False, 2)
-        for m in range(mats):
-            weights = weights_of(lefts, m, 2)
+                for m in both:
+                    for r in range(0, rows, 4):
+                        piece = [in_ref[((r + k) * cols + c) * mats + m] for k in range(4)]
+                        keep(m, r * here, c * wide, jnp.concatenate(piece, axis=0), 3)
+            yield
+            gram = pair_gram(2 * p, 3)
+            yield
+            yield from steps(gram, RESTART, True, 3, box)
+            weights = [weights_of(box[0], m, 3) for m in both]
             for c in range(cols):
-                y = applied(weights, m, c * wide, 2)
-                for r in range(rows):
-                    out_ref[(r * cols + c) * mats + m] = y[r * here : (r + 1) * here]
+                for w, m in zip(weights, both):
+                    keep(m, 0, c * wide, applied(w, m, c * wide, 3), 2)
+            yield
+            gram = pair_gram(2 * p, 2)
+            yield
+            yield from steps(gram, ITERS - RESTART, False, 2, box)
+            weights = [weights_of(box[1], m, 2) for m in both]
+            for c in range(cols):
+                for w, m in zip(weights, both):
+                    y = applied(w, m, c * wide, 2)
+                    for r in range(rows):
+                        out_ref[(r * cols + c) * mats + m] = y[r * here : (r + 1) * here]
+            yield
+
+        for _ in zip(*[pair(p) for p in range(mats // 2)]):
+            pass
         kept_copy.wait()
 
     def call(pieces, kept):
@@ -158,7 +167,7 @@
             in_specs=[pl.BlockSpec(memory_space=pltpu.VMEM)] * 2,
             out_specs=(pl.BlockSpec(memory_space=pltpu.VMEM), pl.BlockSpec(memory_space=pltpu.HBM)),
             scratch_shapes=[
-                pltpu.VMEM((mats, 3 * here * rows, wide * cols), BF16),
+                *[pltpu.VMEM((3 * here * rows, wide * cols), BF16)] * mats,
                 pltpu.SemaphoreType.DMA,
             ],
             compiler_params=pltpu.CompilerParams(vmem_limit_bytes=32 * 1024 * 1024),

time: 88.2 us -> 88.2 us (level)
  no operation moved by 1% of the time
where the time goes in v9:
time: 88.2 us; the launch traced here: 88 us
  blocking collectives  78.9 us (89%)
  Pallas kernels  8.51 us (10%)
    all_to_all x1, blocking collectives, on_device(): lax.all_to_all(new_momentum, axes, split_axis=0, concat_axis=0, tiled=True)  42.9 us
    all_to_all x1, blocking collectives, on_device(): back = lax.all_to_all(pieces, axes, split_axis=0, concat_axis=0, tiled=True)  36 us
    pallas_call x1, Pallas kernels, call(): pl.pallas_call(body, out_shape=(jax.ShapeDtypeStruct(pieces.shape, pieces...  4.8 us
    pallas_call x1, Pallas kernels, fresh_momentum(): pl.pallas_call(body, out_shape=pltpu.VMEM(grad_stack.shape, F32), in_spec...  2.31 us

profile of v9, /device:TPU:0, one launch (start us, length us, event | category | flops | bytes accessed | tf_op | source)
XLA Modules:
  0.0 88.0 jit_solution(98103210283056184)
XLA Ops:
  0.6 2.3 %fresh_momentum.1.kept_ref = f32[512,4,256]{2,1,0:T(4,128)S(1)} custom-call(f32[512,4,256]{2,1,0:T(4,128)} %grad_ref.1, f32[512,4,256]{2,1,0:T(4,128)} %moment_ref.1), custom_call_target="tpu_custom_call" | custom-call | tf_op jit(solution)/shard_map/fresh_momentum/pallas_call | solution.py:203
  2.9 42.9 %all_to_all.10.in_ref = f32[512,4,256]{2,1,0:T(4,128)S(1)} all-to-all(f32[512,4,256]{2,1,0:T(4,128)S(1)} %fresh_momentum.1.kept_ref), channel_id=1, replica_groups=mesh['rows'=16,'cols'=8] {'rows','cols'}, dimensions={0} | all-to-all | bytes 4194304 | tf_op jit(solution)/shard_map/all_to_all | solution.py:248
  45.8 4.8 %orthogonal.1 = (f32[512,4,256]{2,1,0:T(4,128)S(1)}, f32[512,4,256]{2,1,0:T(4,128)}) custom-call(f32[512,4,256]{2,1,0:T(4,128)S(1)} %all_to_all.10.in_ref, f32[512,4,256]{2,1,0:T(4,128)S(1)} %fresh_momentum.1.kept_ref), custom_call_target="tpu_custom_call" | custom-call | tf_op jit(solution)/shard_map/orthogonal/pallas_call | solution.py:161
  50.6 0.0 copy-start
  50.6 36.0 %all_to_all.11.back_ref = f32[512,4,256]{2,1,0:T(4,128)S(1)} all-to-all(f32[512,4,256]{2,1,0:T(4,128)S(1)} %get-tuple-element.4), channel_id=1, replica_groups=mesh['rows'=16,'cols'=8] {'rows','cols'}, dimensions={0} | all-to-all | bytes 4194304 | tf_op jit(solution)/shard_map/all_to_all | solution.py:250
  86.6 0.0 copy-done
  86.6 1.4 %stepped.1 = f32[512,4,256]{2,1,0:T(4,128)} custom-call(f32[512,4,256]{2,1,0:T(4,128)S(1)} %copy-done, f32[512,4,256]{2,1,0:T(4,128)S(1)} %all_to_all.11.back_ref), custom_call_target="tpu_custom_call" | custom-call | tf_op jit(solution)/shard_map/stepped/pallas_call | solution.py:233
Async XLA Ops:
  50.6 36.0 %copy-start = (f32[512,4,256]{2,1,0:T(4,128)S(1)}, f32[512,4,256]{2,1,0:T(4,128)}, u32[]{:S(2)}) copy-start(f32[512,4,256]{2,1,0:T(4,128)} %weight_ref.1) | copy-start | bytes 6291460

commit v10 on v7

--- a/solution.py
+++ b/solution.py
@@ -31,7 +31,7 @@
 
 
 def orthogonal(rows, cols, mats):
-    def body(in_ref, kept_ref, out_ref, kept_out_ref, x_ref, written):
+    def body(in_ref, kept_ref, far_ref, out_ref, kept_out_ref, near_ref, x_ref, written, fetched):
         here, wide = in_ref.shape[1], in_ref.shape[2]
         side = here * rows
         lane = lax.broadcasted_iota(jnp.int32, (side, 2 * side), 1)
@@ -128,6 +128,8 @@
 
         kept_copy = pltpu.make_async_copy(kept_ref, kept_out_ref, written)
         kept_copy.start()
+        fetch = pltpu.make_async_copy(far_ref, near_ref, fetched)
+        fetch.start()
         for m in range(mats):
             for r in range(0, rows, 4):
                 for c in range(cols):
@@ -146,24 +148,31 @@
                 for r in range(rows):
                     out_ref[(r * cols + c) * mats + m] = y[r * here : (r + 1) * here]
         kept_copy.wait()
-
-    def call(pieces, kept):
+        fetch.wait()
+
+    def call(pieces, kept, far):
         n, here, wide = pieces.shape
         return pl.pallas_call(
             body,
             out_shape=(
                 jax.ShapeDtypeStruct(pieces.shape, pieces.dtype),
                 jax.ShapeDtypeStruct(kept.shape, kept.dtype),
+                pltpu.VMEM(far.shape, far.dtype),
             ),
-            in_specs=[pl.BlockSpec(memory_space=pltpu.VMEM)] * 2,
-            out_specs=(pl.BlockSpec(memory_space=pltpu.VMEM), pl.BlockSpec(memory_space=pltpu.HBM)),
+            in_specs=[pl.BlockSpec(memory_space=pltpu.VMEM)] * 2 + [pl.BlockSpec(memory_space=pltpu.HBM)],
+            out_specs=(
+                pl.BlockSpec(memory_space=pltpu.VMEM),
+                pl.BlockSpec(memory_space=pltpu.HBM),
+                pl.BlockSpec(memory_space=pltpu.VMEM),
+            ),
             scratch_shapes=[
                 pltpu.VMEM((mats, 3 * here * rows, wide * cols), BF16),
+                pltpu.SemaphoreType.DMA,
                 pltpu.SemaphoreType.DMA,
             ],
             compiler_params=pltpu.CompilerParams(vmem_limit_bytes=32 * 1024 * 1024),
             name="orthogonal",
-        )(pieces, kept)
+        )(pieces, kept, far)
 
     return call
 
@@ -237,9 +246,9 @@
     rows, cols = lax.axis_size("rows"), lax.axis_size("cols")
     new_momentum = fresh_momentum(grad_stack, moment_stack)
     pieces = lax.all_to_all(new_momentum, axes, split_axis=0, concat_axis=0, tiled=True)
-    pieces, written = orthogonal(rows, cols, pieces.shape[0] // (rows * cols))(pieces, new_momentum)
+    pieces, written, weights = orthogonal(rows, cols, pieces.shape[0] // (rows * cols))(pieces, new_momentum, weight_stack)
     back = lax.all_to_all(pieces, axes, split_axis=0, concat_axis=0, tiled=True)
-    return (stepped(weight_stack, back), written)
+    return (stepped(weights, back), written)
 
 
 def solution(mesh):

time: 88.2 us -> 88.2 us (level)
  no operation moved by 1% of the time
where the time goes in v10:
time: 88.2 us; the launch traced here: 88.1 us
  blocking collectives  78.7 us (89%)
  Pallas kernels  8.7 us (10%)
    all_to_all x1, blocking collectives, on_device(): lax.all_to_all(new_momentum, axes, split_axis=0, concat_axis=0, tiled=True)  42.9 us
    all_to_all x1, blocking collectives, on_device(): back = lax.all_to_all(pieces, axes, split_axis=0, concat_axis=0, tiled=True)  35.9 us
    pallas_call x1, Pallas kernels, call(): pl.pallas_call(body, out_shape=(jax.ShapeDtypeStruct(pieces.shape, pieces...  4.99 us
    pallas_call x1, Pallas kernels, fresh_momentum(): pl.pallas_call(body, out_shape=pltpu.VMEM(grad_stack.shape, F32), in_spec...  2.31 us

profile of v10, /device:TPU:0, one launch (start us, length us, event | category | flops | bytes accessed | tf_op | source)
XLA Modules:
  0.0 88.1 jit_solution(8841541504008771707)
XLA Ops:
  0.6 2.3 %fresh_momentum.1.kept_ref = f32[512,4,256]{2,1,0:T(4,128)S(1)} custom-call(f32[512,4,256]{2,1,0:T(4,128)} %grad_ref.1, f32[512,4,256]{2,1,0:T(4,128)} %moment_ref.1), custom_call_target="tpu_custom_call" | custom-call | tf_op jit(solution)/shard_map/fresh_momentum/pallas_call | solution.py:203
  2.9 0.0 copy-start
  3.0 42.9 %all_to_all.10.in_ref = f32[512,4,256]{2,1,0:T(4,128)S(1)} all-to-all(f32[512,4,256]{2,1,0:T(4,128)S(1)} %fresh_momentum.1.kept_ref), channel_id=1, replica_groups=mesh['rows'=16,'cols'=8] {'rows','cols'}, dimensions={0} | all-to-all | bytes 4194304 | tf_op jit(solution)/shard_map/all_to_all | solution.py:248
  45.8 0.0 copy-done
  45.8 5.0 %orthogonal.1 = (f32[512,4,256]{2,1,0:T(4,128)S(1)}, f32[512,4,256]{2,1,0:T(4,128)}, f32[512,4,256]{2,1,0:T(4,128)S(1)}) custom-call(f32[512,4,256]{2,1,0:T(4,128)S(1)} %all_to_all.10.in_ref, f32[512,4,256]{2,1,0:T(4,128)S(1)} %fresh_momentum.1.kept_ref, f32[512,4,256]{2,1,0:T(4,128)S(1)} %copy-done), custom_call_target="tpu_custom_call" | custom-call | tf_op jit(solution)/shard_map/orthogonal/pallas_call | solution.py:155
  50.8 35.9 %all_to_all.11.back_ref = f32[512,4,256]{2,1,0:T(4,128)S(1)} all-to-all(f32[512,4,256]{2,1,0:T(4,128)S(1)} %get-tuple-element.6), channel_id=1, replica_groups=mesh['rows'=16,'cols'=8] {'rows','cols'}, dimensions={0} | all-to-all | bytes 4194304 | tf_op jit(solution)/shard_map/all_to_all | solution.py:250
  86.7 1.4 %stepped.1 = f32[512,4,256]{2,1,0:T(4,128)} custom-call(f32[512,4,256]{2,1,0:T(4,128)S(1)} %get-tuple-element.5.weight_ref, f32[512,4,256]{2,1,0:T(4,128)S(1)} %all_to_all.11.back_ref), custom_call_target="tpu_custom_call" | custom-call | tf_op jit(solution)/shard_map/stepped/pallas_call | solution.py:233
Async XLA Ops:
  2.9 42.9 %copy-start = (f32[512,4,256]{2,1,0:T(4,128)S(1)}, f32[512,4,256]{2,1,0:T(4,128)}, u32[]{:S(2)}) copy-start(f32[512,4,256]{2,1,0:T(4,128)} %far_ref.1) | copy-start | bytes 6291460
